TPU v7x, 256 devices: a whole 4x4x8 slice. The times are simulated.
256 devices in a mesh: row: 32 (over x, z_lo, y), col: 8 (over z_hi, core).
Axes of the slice: x: 4, y: 4, z: 8 (z_hi: 4, z_lo: 2; z = z_hi * 2 + z_lo), core: 2. Of those that a mesh axis runs over, the one named last changes fastest.
Arguments:
- adj_tiles: bfloat16 [32, 8, 128, 128, 128], P('row', 'col'), may hold values from 0 to 1, as said below
- tile_rows: int32 [32, 8, 128], P('row', 'col'), may hold values from 0 to 7, as said below
- tile_cols: int32 [32, 8, 128], P('row', 'col'), may hold values from 0 to 31, as said below
- tile_count: int32 [32, 8], P('row', 'col'), may hold values from 1 to 128, as said below
- tile_depth: int32 [256, 128], P(('row', 'col')), may hold values from 1 to 7, as said below
- source_ids: int32 [128], replicated, may hold values from 0 to 32767
Outputs:
- path_sums: float32 [32768, 128], P(('row', 'col'))
- log_scales: float32 [6, 128], replicated
Inputs may be any that keep to these rules, and one draw needn't show every extreme that they name: `adj_tiles`: every entry is 0 or 1. The live slots of a device are its first tile_count slots; at least one device holds 128 live slots. `tile_rows`: slots past a device's live count carry 0. `tile_cols`: slots past a device's live count carry 0. `tile_depth`: the value 6 + 1 marks a tile that takes path counts at every level.
All inputs are finite; a program needn't handle non-finite values.
Results may differ from a plain program's by a relative error of at most 0.0003.
Values may be sent and summed in bfloat16 or wider, within the bound.
A program may use at most 64 MiB of HBM per device.

v0:
```python
import functools

import jax
import jax.numpy as jnp
from jax import lax
from jax.sharding import Mesh
from jax.sharding import PartitionSpec as P

TILE = 128
LEVELS = 6
ROW = ("row_0", "row_1", "row_2")
COL = ("col_0", "col_1")
ROW_COL = ("row_0", "row_1", "row_2", "col_0", "col_1")


EPSILON = 1e-06


def joined_along(parts, dim):
    lengths = list(parts.shape[1:])
    lengths[dim] *= parts.shape[0]
    return jnp.moveaxis(parts, 0, dim).reshape(lengths)


def copy_for_each(shard, axis):
    copies = jnp.broadcast_to(shard, (lax.axis_size(axis), *shard.shape))
    return lax.all_to_all(copies, axis, split_axis=0, concat_axis=0, tiled=True)


def collect(shard, axis, dim):
    return joined_along(copy_for_each(shard, axis), dim)


def cut_along(shard, dim, count):
    before, after = (shard.shape[:dim], shard.shape[dim + 1 :])
    return jnp.moveaxis(shard.reshape(*before, count, -1, *after), dim, 0)


def sent_and_summed(shard, axis, dim):
    count = lax.axis_size(axis)
    parts = lax.all_to_all(cut_along(shard, dim, count), axis, 0, 0, tiled=True)
    return jnp.sum(parts, axis=0)


def one_axis_at_a_time(shard, axes):
    return functools.reduce(lax.psum, axes, shard)


def tile_products(running, blocks, row_ids, col_ids, sources, base_tile, first_slot, end_slot):
    slot_total = blocks.shape[0]
    batch_size = min(16, slot_total)
    turn_count = (jnp.maximum(end_slot - first_slot, 0) + batch_size - 1) // batch_size

    def one_turn(turn_index, summed):
        wanted_start = first_slot + turn_index * batch_size
        window = jnp.minimum(wanted_start, slot_total - batch_size)
        part_blocks = lax.dynamic_slice_in_dim(blocks, window, batch_size, 0)
        part_rows = lax.dynamic_slice_in_dim(row_ids, window, batch_size, 0)
        part_cols = lax.dynamic_slice_in_dim(col_ids, window, batch_size, 0)
        slot_ids = window + jnp.arange(batch_size, dtype=jnp.int32)
        wanted = (slot_ids >= wanted_start) & (slot_ids < end_slot)
        local_cols = jnp.clip(part_cols - base_tile, 0, sources.shape[0] - 1)
        picked = jnp.take(sources, local_cols, axis=0)
        products = jnp.einsum(
            "gij,gjs->gis", part_blocks, picked, preferred_element_type=jnp.float32
        )
        return summed.at[part_rows].add(products * wanted.astype(jnp.float32)[:, None, None])

    return lax.fori_loop(0, turn_count, one_turn, running)


def local(adj_tiles, tile_rows, tile_cols, tile_count, tile_depth, source_ids):
    blocks = adj_tiles[0, 0]
    row_ids = tile_rows[0, 0]
    col_ids = tile_cols[0, 0]
    live_count = tile_count[0, 0]
    row_total = lax.axis_size(ROW)
    col_total = lax.axis_size(COL)
    piece_tiles = tile_depth.shape[0]
    panel_width = tile_depth.shape[1]
    piece_rows = piece_tiles * TILE
    dest_tiles = col_total * piece_tiles
    src_tiles = row_total * piece_tiles
    vertex_total = piece_rows * row_total * col_total
    position = lax.axis_index(ROW) * col_total + lax.axis_index(COL)
    vertex_ids = position * piece_rows + jnp.arange(piece_rows, dtype=jnp.int32)
    start_panel = (vertex_ids[:, None] == source_ids[None, :]).astype(jnp.float32)
    tile_lists = [(blocks, row_ids, col_ids, live_count)]
    zero_sums = jnp.zeros((dest_tiles, TILE, panel_width), jnp.float32)
    path_sums = start_panel
    frontier = start_panel.astype(jnp.bfloat16)
    log_scales = []
    for level_index in range(1, LEVELS + 1):
        gathered = collect(frontier, ROW, 0)
        sources = gathered.reshape(src_tiles, TILE, panel_width)
        partials = tuple(
            (
                tile_products(
                    zero_sums, tile_list[0], tile_list[1], tile_list[2], sources, 0, 0, tile_list[3]
                )
                for tile_list in tile_lists
            )
        )
        combined = partials[0]
        reduced = sent_and_summed(combined.reshape(dest_tiles * TILE, panel_width), COL, 0)
        reached = (tile_depth >= level_index).astype(jnp.float32)
        raw_paths = (reduced.reshape(piece_tiles, TILE, panel_width) * reached[:, None, :]).reshape(
            piece_rows, panel_width
        )
        squares = one_axis_at_a_time(jnp.sum(raw_paths * raw_paths, axis=0), ROW_COL)
        mean_square = squares / vertex_total + EPSILON
        scaled = raw_paths * lax.rsqrt(mean_square)
        path_sums = path_sums + scaled
        log_scales.append(0.5 * jnp.log(mean_square))
        frontier = scaled.astype(jnp.bfloat16)
    return (path_sums, jnp.stack(log_scales))


def solution(mesh):
    split = Mesh(mesh.devices.reshape(4, 2, 4, 4, 2), ("row_0", "row_1", "row_2", "col_0", "col_1"))
    in_specs = (
        P(ROW, COL, None, None, None),
        P(ROW, COL, None),
        P(ROW, COL, None),
        P(ROW, COL),
        P(ROW_COL, None),
        P(),
    )
    out_specs = (P(ROW_COL, None), P())
    return jax.shard_map(local, mesh=split, in_specs=in_specs, out_specs=out_specs, check_vma=False)
```

profile of v0, /device:TPU:1, one launch (start us, length us, event | category | flops | bytes accessed | tf_op | source)
XLA Modules:
  0.0 749.8 jit_solution(16349796312365457652)
XLA Ops:
  2.6 9.2 %all-to-all-start = ((bf16[32,128,128]{2,1,0:T(8,128)(2,1)}), bf16[32,128,128]{2,1,0:T(8,128)(2,1)S(1)}, u32[]{:S(2)}, u32[]{:S(2)}) async-start(bf16[32,128,128]{2,1,0:T(8,128)(2,1)} %broadcast_in_dim.46), calls=%async_computation | async-start | bytes 2097152 | tf_op jit(solution)/shard_map/all_to_all | solution.py:27
  12.5 14.9 %all-to-all-done = bf16[32,128,128]{2,1,0:T(8,128)(2,1)S(1)} async-done(((bf16[32,128,128]{2,1,0:T(8,128)(2,1)}), bf16[32,128,128]{2,1,0:T(8,128)(2,1)S(1)}, u32[]{:S(2)}, u32[]{:S(2)}) %all-to-all-start) | async-done | bytes 1048608 | tf_op jit(solution)/shard_map/all_to_all | solution.py:27
  28.2 22.8 %while.60 = (s32[]{:T(128)}, f32[8,128,128]{2,1,0:T(8,128)}, s32[]{:T(128)}, s32[128]{0:T(128)}, bf16[128,128,128]{2,1,0:T(8,128)(2,1)}, /*index=5*/s32[128]{0:T...) while((s32[]{:T(128)}, f32[8,128,128]{2,1,0:T(8,128)}, ...), condition=%wide.region_2.4_spmd, body=%wide.region_0.3_spmd.sunk | while | flops 67896568 | bytes 6296367 | solution.py:69
  51.0 47.0 %all-to-all-start.1 = ((f32[8,128,128]{2,1,0:T(8,128)}), f32[8,128,128]{2,1,0:T(8,128)S(1)}, u32[]{:S(2)}, u32[]{:S(2)}) async-start(f32[8,128,128]{2,1,0:T(8,128)} %get-tuple-element.261), calls=%async_computation.1 | async-start | bytes 1048576 | tf_op jit(solution)/shard_map/all_to_all | solution.py:41
  98.0 13.0 %all-to-all-done.1 = f32[8,128,128]{2,1,0:T(8,128)S(1)} async-done(((f32[8,128,128]{2,1,0:T(8,128)}), f32[8,128,128]{2,1,0:T(8,128)S(1)}, u32[]{:S(2)}, u32[]{:S(2)}) %all-to-all-start.1) | async-done | bytes 524320 | tf_op jit(solution)/shard_map/all_to_all | solution.py:41
  111.1 7.2 psum.210
  118.4 5.5 psum.211
  123.9 6.5 psum.212
  130.4 7.1 psum.213
  137.5 11.4 %psum.214 = f32[128]{0:T(128)S(1)} all-reduce(f32[128]{0:T(128)S(1)} %psum.213), channel_id=1, replica_groups=mesh['row_0'=4,'row_1'=2,'row_2'=4,'col_0'=4,'col_1'=2] {'col_1'}, use_global_device_ids=true, to_apply=%region_9.11 | all-reduce | flops 128 | bytes 1024 | tf_op jit(solution)/shard_map/psum | solution.py:46
  154.0 15.7 %all-to-all-done.2 = bf16[32,128,128]{2,1,0:T(8,128)(2,1)S(1)} async-done(((bf16[32,128,128]{2,1,0:T(8,128)(2,1)}), bf16[32,128,128]{2,1,0:T(8,128)(2,1)S(1)}, u32[]{:S(2)}, u32[]{:S(2)}) %all-to-all-start.2) | async-done | bytes 1048608 | tf_op jit(solution)/shard_map/all_to_all | solution.py:27
  169.8 15.6 %while.61 = (s32[]{:T(128)}, f32[8,128,128]{2,1,0:T(8,128)S(1)}, s32[]{:T(128)}, s32[128]{0:T(128)}, bf16[128,128,128]{2,1,0:T(8,128)(2,1)}, /*index=5*/s32[128]...) while((s32[]{:T(128)}, f32[8,128,128]{2,1,0:T(8,128)S(1)}, ...), condition=%wide.region_12.14_spmd, body=%wide.region_10.13_spmd.sunk | while | flops 67896568 | bytes 6296367 | solution.py:69
  185.3 46.7 %all_to_all.60 = f32[8,128,128]{2,1,0:T(8,128)S(1)} all-to-all(f32[8,128,128]{2,1,0:T(8,128)S(1)} %get-tuple-element.262), channel_id=1, replica_groups=mesh['row_0'=4,'row_1'=2,'row_2'=4,'col_0'=4,'col_1'=2] {'col_0','col_1'}, dimensions={0} | all-to-all | bytes 1048576 | tf_op jit(solution)/shard_map/all_to_all | solution.py:41
  232.1 7.8 %psum.215 = f32[128]{0:T(128)S(1)} all-reduce(f32[128]{0:T(128)S(1)} %multiply_reduce_fusion.4), channel_id=1, replica_groups=mesh['row_0'=4,'row_1'=2,'row_2'=4,'col_0'=4,'col_1'=2] {'row_0'}, use_global_device_ids=true, to_apply=%region_15.17 | all-reduce | flops 128 | bytes 1024 | tf_op jit(solution)/shard_map/psum | solution.py:46
  243.7 6.0 psum.217
  249.6 8.7 %psum.218 = f32[128]{0:T(128)S(1)} all-reduce(f32[128]{0:T(128)S(1)} %psum.217), channel_id=1, replica_groups=mesh['row_0'=4,'row_1'=2,'row_2'=4,'col_0'=4,'col_1'=2] {'col_0'}, use_global_device_ids=true, to_apply=%region_18.20 | all-reduce | flops 128 | bytes 1024 | tf_op jit(solution)/shard_map/psum | solution.py:46
  258.3 10.2 %psum.219 = f32[128]{0:T(128)S(1)} all-reduce(f32[128]{0:T(128)S(1)} %psum.218), channel_id=1, replica_groups=mesh['row_0'=4,'row_1'=2,'row_2'=4,'col_0'=4,'col_1'=2] {'col_1'}, use_global_device_ids=true, to_apply=%region_19.21 | all-reduce | flops 128 | bytes 1024 | tf_op jit(solution)/shard_map/psum | solution.py:46
  273.7 15.8 %all-to-all-done.4 = bf16[32,128,128]{2,1,0:T(8,128)(2,1)S(1)} async-done(((bf16[32,128,128]{2,1,0:T(8,128)(2,1)}), bf16[32,128,128]{2,1,0:T(8,128)(2,1)S(1)}, u32[]{:S(2)}, u32[]{:S(2)}) %all-to-all-start.4) | async-done | bytes 1048608 | tf_op jit(solution)/shard_map/all_to_all | solution.py:27
  289.5 15.6 %while.62 = (s32[]{:T(128)}, f32[8,128,128]{2,1,0:T(8,128)S(1)}, s32[]{:T(128)}, s32[128]{0:T(128)}, bf16[128,128,128]{2,1,0:T(8,128)(2,1)}, /*index=5*/s32[128]...) while((s32[]{:T(128)}, f32[8,128,128]{2,1,0:T(8,128)S(1)}, ...), condition=%wide.region_22.24_spmd, body=%wide.region_20.23_spmd.sunk | while | flops 67896568 | bytes 6296367 | solution.py:69
  305.1 46.5 %all_to_all.61 = f32[8,128,128]{2,1,0:T(8,128)S(1)} all-to-all(f32[8,128,128]{2,1,0:T(8,128)S(1)} %get-tuple-element.263), channel_id=1, replica_groups=mesh['row_0'=4,'row_1'=2,'row_2'=4,'col_0'=4,'col_1'=2] {'col_0','col_1'}, dimensions={0} | all-to-all | bytes 1048576 | tf_op jit(solution)/shard_map/all_to_all | solution.py:41
  351.7 7.8 %psum.220 = f32[128]{0:T(128)S(1)} all-reduce(f32[128]{0:T(128)S(1)} %multiply_reduce_fusion.3), channel_id=1, replica_groups=mesh['row_0'=4,'row_1'=2,'row_2'=4,'col_0'=4,'col_1'=2] {'row_0'}, use_global_device_ids=true, to_apply=%region_25.27 | all-reduce | flops 128 | bytes 1024 | tf_op jit(solution)/shard_map/psum | solution.py:46
  363.3 6.1 psum.222
  369.3 8.5 %psum.223 = f32[128]{0:T(128)S(1)} all-reduce(f32[128]{0:T(128)S(1)} %psum.222), channel_id=1, replica_groups=mesh['row_0'=4,'row_1'=2,'row_2'=4,'col_0'=4,'col_1'=2] {'col_0'}, use_global_device_ids=true, to_apply=%region_28.30 | all-reduce | flops 128 | bytes 1024 | tf_op jit(solution)/shard_map/psum | solution.py:46
  377.8 9.6 %psum.224 = f32[128]{0:T(128)S(1)} all-reduce(f32[128]{0:T(128)S(1)} %psum.223), channel_id=1, replica_groups=mesh['row_0'=4,'row_1'=2,'row_2'=4,'col_0'=4,'col_1'=2] {'col_1'}, use_global_device_ids=true, to_apply=%region_29.31 | all-reduce | flops 128 | bytes 1024 | tf_op jit(solution)/shard_map/psum | solution.py:46
  388.7 4.3 all-to-all-start.6
  392.9 15.5 %all-to-all-done.6 = bf16[32,128,128]{2,1,0:T(8,128)(2,1)S(1)} async-done(((bf16[32,128,128]{2,1,0:T(8,128)(2,1)}), bf16[32,128,128]{2,1,0:T(8,128)(2,1)S(1)}, u32[]{:S(2)}, u32[]{:S(2)}) %all-to-all-start.6) | async-done | bytes 1048608 | tf_op jit(solution)/shard_map/all_to_all | solution.py:27
  408.5 15.6 %while.63 = (s32[]{:T(128)}, f32[8,128,128]{2,1,0:T(8,128)S(1)}, s32[]{:T(128)}, s32[128]{0:T(128)}, bf16[128,128,128]{2,1,0:T(8,128)(2,1)}, /*index=5*/s32[128]...) while((s32[]{:T(128)}, f32[8,128,128]{2,1,0:T(8,128)S(1)}, ...), condition=%wide.region_32.34_spmd, body=%wide.region_30.33_spmd.sunk | while | flops 67896568 | bytes 6296367 | solution.py:69
  424.1 46.7 %all_to_all.62 = f32[8,128,128]{2,1,0:T(8,128)S(1)} all-to-all(f32[8,128,128]{2,1,0:T(8,128)S(1)} %get-tuple-element.264), channel_id=1, replica_groups=mesh['row_0'=4,'row_1'=2,'row_2'=4,'col_0'=4,'col_1'=2] {'col_0','col_1'}, dimensions={0} | all-to-all | bytes 1048576 | tf_op jit(solution)/shard_map/all_to_all | solution.py:41
  470.8 8.1 %psum.225 = f32[128]{0:T(128)S(1)} all-reduce(f32[128]{0:T(128)S(1)} %multiply_reduce_fusion.2), channel_id=1, replica_groups=mesh['row_0'=4,'row_1'=2,'row_2'=4,'col_0'=4,'col_1'=2] {'row_0'}, use_global_device_ids=true, to_apply=%region_35.37 | all-reduce | flops 128 | bytes 1024 | tf_op jit(solution)/shard_map/psum | solution.py:46
  482.7 6.1 psum.227
  488.8 8.4 %psum.228 = f32[128]{0:T(128)S(1)} all-reduce(f32[128]{0:T(128)S(1)} %psum.227), channel_id=1, replica_groups=mesh['row_0'=4,'row_1'=2,'row_2'=4,'col_0'=4,'col_1'=2] {'col_0'}, use_global_device_ids=true, to_apply=%region_38.40 | all-reduce | flops 128 | bytes 1024 | tf_op jit(solution)/shard_map/psum | solution.py:46
  497.1 10.1 %psum.229 = f32[128]{0:T(128)S(1)} all-reduce(f32[128]{0:T(128)S(1)} %psum.228), channel_id=1, replica_groups=mesh['row_0'=4,'row_1'=2,'row_2'=4,'col_0'=4,'col_1'=2] {'col_1'}, use_global_device_ids=true, to_apply=%region_39.41 | all-reduce | flops 128 | bytes 1024 | tf_op jit(solution)/shard_map/psum | solution.py:46
  508.4 4.1 all-to-all-start.8
  512.6 15.8 %all-to-all-done.8 = bf16[32,128,128]{2,1,0:T(8,128)(2,1)S(1)} async-done(((bf16[32,128,128]{2,1,0:T(8,128)(2,1)}), bf16[32,128,128]{2,1,0:T(8,128)(2,1)S(1)}, u32[]{:S(2)}, u32[]{:S(2)}) %all-to-all-start.8) | async-done | bytes 1048608 | tf_op jit(solution)/shard_map/all_to_all | solution.py:27
  528.4 15.6 %while.64 = (s32[]{:T(128)}, f32[8,128,128]{2,1,0:T(8,128)S(1)}, s32[]{:T(128)}, s32[128]{0:T(128)}, bf16[128,128,128]{2,1,0:T(8,128)(2,1)}, /*index=5*/s32[128]...) while((s32[]{:T(128)}, f32[8,128,128]{2,1,0:T(8,128)S(1)}, ...), condition=%wide.region_42.44_spmd, body=%wide.region_40.43_spmd.sunk | while | flops 67896568 | bytes 6296367 | solution.py:69
  544.0 46.9 %all_to_all.63 = f32[8,128,128]{2,1,0:T(8,128)S(1)} all-to-all(f32[8,128,128]{2,1,0:T(8,128)S(1)} %get-tuple-element.265), channel_id=1, replica_groups=mesh['row_0'=4,'row_1'=2,'row_2'=4,'col_0'=4,'col_1'=2] {'col_0','col_1'}, dimensions={0} | all-to-all | bytes 1048576 | tf_op jit(solution)/shard_map/all_to_all | solution.py:41
  590.9 8.1 %psum.230 = f32[128]{0:T(128)S(1)} all-reduce(f32[128]{0:T(128)S(1)} %multiply_reduce_fusion.1), channel_id=1, replica_groups=mesh['row_0'=4,'row_1'=2,'row_2'=4,'col_0'=4,'col_1'=2] {'row_0'}, use_global_device_ids=true, to_apply=%region_45.47 | all-reduce | flops 128 | bytes 1024 | tf_op jit(solution)/shard_map/psum | solution.py:46
  602.8 6.0 psum.232
  608.7 8.0 %psum.233 = f32[128]{0:T(128)S(1)} all-reduce(f32[128]{0:T(128)S(1)} %psum.232), channel_id=1, replica_groups=mesh['row_0'=4,'row_1'=2,'row_2'=4,'col_0'=4,'col_1'=2] {'col_0'}, use_global_device_ids=true, to_apply=%region_48.50 | all-reduce | flops 128 | bytes 1024 | tf_op jit(solution)/shard_map/psum | solution.py:46
  616.7 10.5 %psum.234 = f32[128]{0:T(128)S(1)} all-reduce(f32[128]{0:T(128)S(1)} %psum.233), channel_id=1, replica_groups=mesh['row_0'=4,'row_1'=2,'row_2'=4,'col_0'=4,'col_1'=2] {'col_1'}, use_global_device_ids=true, to_apply=%region_49.51 | all-reduce | flops 128 | bytes 1024 | tf_op jit(solution)/shard_map/psum | solution.py:46
  633.1 15.8 %all-to-all-done.10 = bf16[32,128,128]{2,1,0:T(8,128)(2,1)S(1)} async-done(((bf16[32,128,128]{2,1,0:T(8,128)(2,1)}), bf16[32,128,128]{2,1,0:T(8,128)(2,1)S(1)}, u32[]{:S(2)}, u32[]{:S(2)}) %all-to-all-start.10) | async-done | bytes 1048608 | tf_op jit(solution)/shard_map/all_to_all | solution.py:27
  648.9 15.6 %while.65 = (s32[]{:T(128)}, f32[8,128,128]{2,1,0:T(8,128)S(1)}, s32[]{:T(128)}, s32[128]{0:T(128)}, bf16[128,128,128]{2,1,0:T(8,128)(2,1)}, /*index=5*/s32[128]...) while((s32[]{:T(128)}, f32[8,128,128]{2,1,0:T(8,128)S(1)}, ...), condition=%wide.region_52.54_spmd, body=%wide.region_50.53_spmd.sunk | while | flops 67896568 | bytes 6296367 | solution.py:69
  664.5 46.9 %all_to_all.64 = f32[8,128,128]{2,1,0:T(8,128)S(1)} all-to-all(f32[8,128,128]{2,1,0:T(8,128)S(1)} %get-tuple-element.266), channel_id=1, replica_groups=mesh['row_0'=4,'row_1'=2,'row_2'=4,'col_0'=4,'col_1'=2] {'col_0','col_1'}, dimensions={0} | all-to-all | bytes 1048576 | tf_op jit(solution)/shard_map/all_to_all | solution.py:41
  711.4 6.0 psum.235
  717.4 4.8 psum.236
  722.2 6.8 psum.237
  729.0 8.4 %psum.238 = f32[128]{0:T(128)S(1)} all-reduce(f32[128]{0:T(128)S(1)} %psum.237), channel_id=1, replica_groups=mesh['row_0'=4,'row_1'=2,'row_2'=4,'col_0'=4,'col_1'=2] {'col_0'}, use_global_device_ids=true, to_apply=%region_58.60 | all-reduce | flops 128 | bytes 1024 | tf_op jit(solution)/shard_map/psum | solution.py:46
  737.4 10.3 %psum.239 = f32[128]{0:T(128)S(1)} all-reduce(f32[128]{0:T(128)S(1)} %psum.238), channel_id=1, replica_groups=mesh['row_0'=4,'row_1'=2,'row_2'=4,'col_0'=4,'col_1'=2] {'col_1'}, use_global_device_ids=true, to_apply=%region_59.61 | all-reduce | flops 128 | bytes 1024 | tf_op jit(solution)/shard_map/psum | solution.py:46
  (161 shorter events, 138.8 us)
Async XLA Ops:
  2.6 24.7 %all-to-all-start = ((bf16[32,128,128]{2,1,0:T(8,128)(2,1)}), bf16[32,128,128]{2,1,0:T(8,128)(2,1)S(1)}, u32[]{:S(2)}, u32[]{:S(2)}) async-start(bf16[32,128,128]{2,1,0:T(8,128)(2,1)} %broadcast_in_dim.46), calls=%async_computation | async-start | bytes 2097152 | tf_op jit(solution)/shard_map/all_to_all | solution.py:27
  28.2 69.8 %copy-start.2 = (s32[1,128]{1,0:T(1,128)S(1)}, s32[1,128]{1,0:T(1,128)}, u32[]{:S(2)}) copy-start(s32[1,128]{1,0:T(1,128)} %param.24) | copy-start | bytes 1540
  51.0 118.8 %copy-start = (s32[128]{0:T(128)S(1)}, s32[128]{0:T(128)}, u32[]{:S(2)}) copy-start(s32[128]{0:T(128)} %get-tuple-element.981) | copy-start | bytes 1540
  51.0 60.1 %all-to-all-start.1 = ((f32[8,128,128]{2,1,0:T(8,128)}), f32[8,128,128]{2,1,0:T(8,128)S(1)}, u32[]{:S(2)}, u32[]{:S(2)}) async-start(f32[8,128,128]{2,1,0:T(8,128)} %get-tuple-element.261), calls=%async_computation.1 | async-start | bytes 1048576 | tf_op jit(solution)/shard_map/all_to_all | solution.py:41
  150.1 19.6 %all-to-all-start.2 = ((bf16[32,128,128]{2,1,0:T(8,128)(2,1)}), bf16[32,128,128]{2,1,0:T(8,128)(2,1)S(1)}, u32[]{:S(2)}, u32[]{:S(2)}) async-start(bf16[32,128,128]{2,1,0:T(8,128)(2,1)} %broadcast_in_dim.49), calls=%async_computation.2 | async-start | bytes 2097152 | tf_op jit(solution)/shard_map/all_to_all | solution.py:27
  269.8 19.7 %all-to-all-start.4 = ((bf16[32,128,128]{2,1,0:T(8,128)(2,1)}), bf16[32,128,128]{2,1,0:T(8,128)(2,1)S(1)}, u32[]{:S(2)}, u32[]{:S(2)}) async-start(bf16[32,128,128]{2,1,0:T(8,128)(2,1)} %broadcast_in_dim.50), calls=%async_computation.4 | async-start | bytes 2097152 | tf_op jit(solution)/shard_map/all_to_all | solution.py:27
  388.7 19.8 %all-to-all-start.6 = ((bf16[32,128,128]{2,1,0:T(8,128)(2,1)}), bf16[32,128,128]{2,1,0:T(8,128)(2,1)S(1)}, u32[]{:S(2)}, u32[]{:S(2)}) async-start(bf16[32,128,128]{2,1,0:T(8,128)(2,1)} %broadcast_in_dim.72), calls=%async_computation.6 | async-start | bytes 2097152 | tf_op jit(solution)/shard_map/all_to_all | solution.py:27
  508.4 19.9 %all-to-all-start.8 = ((bf16[32,128,128]{2,1,0:T(8,128)(2,1)}), bf16[32,128,128]{2,1,0:T(8,128)(2,1)S(1)}, u32[]{:S(2)}, u32[]{:S(2)}) async-start(bf16[32,128,128]{2,1,0:T(8,128)(2,1)} %broadcast_in_dim.73), calls=%async_computation.8 | async-start | bytes 2097152 | tf_op jit(solution)/shard_map/all_to_all | solution.py:27
  629.1 19.7 %all-to-all-start.10 = ((bf16[32,128,128]{2,1,0:T(8,128)(2,1)}), bf16[32,128,128]{2,1,0:T(8,128)(2,1)S(1)}, u32[]{:S(2)}, u32[]{:S(2)}) async-start(bf16[32,128,128]{2,1,0:T(8,128)(2,1)} %broadcast_in_dim.74), calls=%async_computation.10 | async-start | bytes 2097152 | tf_op jit(solution)/shard_map/all_to_all | solution.py:27
  648.9 98.9 %copy-start.1 = (s32[128]{0:T(128)S(1)}, s32[128]{0:T(128)}, u32[]{:S(2)}) copy-start(s32[128]{0:T(128)} %param.25) | copy-start | bytes 1540
where the time goes:
time: 758 us; the launch traced here: 750 us
  blocking collectives  452 us (60%)
  waiting for transfers between devices  106 us (14%)
  starting transfers between devices  76.4 us (10%)
  other arithmetic  65.2 us (9%)
  matrix products  25.5 us (3%)
  local copies, waits for them, and re-layouts  21.3 us (3%)
    all_to_all x5, blocking collectives, sent_and_summed(): parts = lax.all_to_all(cut_along(shard, dim, count), axis, 0, 0, tiled=True)  234 us
    psum x30, blocking collectives, one_axis_at_a_time(): return functools.reduce(lax.psum, axes, shard)  219 us
    all_to_all x6, waiting for transfers between devices, copy_for_each(): return lax.all_to_all(copies, axis, split_axis=0, concat_axis=0, tiled=True)  93.4 us
    all_to_all x1, starting transfers between devices, sent_and_summed(): parts = lax.all_to_all(cut_along(shard, dim, count), axis, 0, 0, tiled=True)  47 us
    scatter-add x18, other arithmetic, one_turn(): summed.at[part_rows]  34.1 us
    all_to_all x6, starting transfers between devices, copy_for_each(): return lax.all_to_all(copies, axis, split_axis=0, concat_axis=0, tiled=True)  29.4 us
    dot_general x18, matrix products, one_turn(): jnp.einsum('gij,gjs->gis', part_blocks, picked, preferred_element_type=jn...  25.5 us
  transfers between devices with their start and end apart: 7, of which 7 were waited for; matrix products, arithmetic and copies ran while one was open for 0% of the time, Pallas kernels for 0%

commit v1 on v0

v1 whole, which is shorter than its diff:
```python
import jax
import jax.numpy as jnp
from jax import lax
from jax.experimental import pallas as pl
from jax.experimental.pallas import tpu as pltpu
from jax.sharding import PartitionSpec as P

MESH = pl.DeviceIdType.MESH
TILE = 128
PANEL = 128
LEVELS = 6
KMAX = 128
DESTS = 8
SRCS = 32
N_ROW = 32
N_COL = 8
VERTICES = 32768
EPSILON = 1e-06
SHRINK = 2.0**-10
CHUNK = 4
CHUNK_K = CHUNK * TILE
LOADS = 8
LOAD_SLOTS = KMAX // LOADS


def place_of(x, z_lo, y):
    return z_lo * 16 + (1 - z_lo) * (x * 4 + y) + z_lo * (y * 4 + x)


def row_of(x, z_lo, y):
    return x * 8 + z_lo * 4 + y


def densify(count_ref, rows_ref, cols_ref, tiles_hbm, dense_ref, tiles, load_sem):
    count = count_ref[0]

    def load(part):
        slots = pl.ds(part * LOAD_SLOTS, LOAD_SLOTS)
        return pltpu.make_async_copy(tiles_hbm.at[slots], tiles.at[slots], load_sem.at[part])

    for part in range(LOADS):
        load(part).start()

    @pl.loop(0, DESTS * TILE // 16)
    def _(block):
        rows = pl.ds(pl.multiple_of(block * 16, 16), 16)
        dense_ref[rows, :] = jnp.zeros((16, SRCS * TILE), jnp.bfloat16)

    for part in range(LOADS):
        load(part).wait()

        @pl.loop(part * LOAD_SLOTS, jnp.minimum(count, (part + 1) * LOAD_SLOTS))
        def _(slot):
            dest = rows_ref[slot]
            row = cols_ref[slot]
            place = place_of(row // 8, (row // 4) % 2, row % 4)
            rows = pl.ds(pl.multiple_of(dest * TILE, TILE), TILE)
            columns = pl.ds(pl.multiple_of(place * TILE, TILE), TILE)
            dense_ref[rows, columns] = dense_ref[rows, columns] + tiles[slot]


def levels_kernel(
    dense,
    depth_ref,
    ids_ref,
    sums_ref,
    logs_ref,
    panel,
    partial,
    from_core,
    combined,
    from_z,
    paths,
    squares,
    squares_col,
    squares_row,
    tile_send,
    tile_recv,
    core_send,
    core_recv,
    z_send,
    z_recv,
    col_send,
    col_recv,
    row_send,
    row_recv,
):
    r = lax.axis_index("row")
    c = lax.axis_index("col")
    x, z_lo, y = r // 8, (r // 4) % 2, r % 4
    z_hi, core = c // 2, c % 2
    my_place = place_of(x, z_lo, y)

    barrier = pltpu.get_barrier_semaphore()

    @pl.loop(1, N_ROW)
    def _(step):
        pl.semaphore_signal(
            barrier, inc=1, device_id={"row": (r + step) % N_ROW, "col": c}, device_id_type=MESH
        )

    @pl.loop(1, N_COL)
    def _(step):
        pl.semaphore_signal(
            barrier, inc=1, device_id={"row": r, "col": (c + step) % N_COL}, device_id_type=MESH
        )

    def multiply(chunk, first):
        columns = pl.ds(pl.multiple_of(chunk * CHUNK_K, CHUNK_K), CHUNK_K)

        def run(buffer):
            source = panel[buffer, pl.ds(pl.multiple_of(chunk * CHUNK, CHUNK), CHUNK)].reshape(CHUNK_K, PANEL)
            for part in range(4):
                product = jnp.dot(
                    dense[part * 256 : (part + 1) * 256, columns], source, preferred_element_type=jnp.float32
                ).reshape(2, TILE, PANEL)
                if first:
                    partial[part * 2 : part * 2 + 2] = product
                else:
                    partial[part * 2 : part * 2 + 2] += product

        return run

    def tile_copy(buffer, place, to_x, to_z, to_y):
        return pltpu.make_async_remote_copy(
            src_ref=panel.at[buffer, place],
            dst_ref=panel.at[buffer, place],
            send_sem=tile_send,
            recv_sem=tile_recv.at[buffer, place],
            device_id={"row": row_of(to_x, to_z, to_y), "col": c},
            device_id_type=MESH,
        )

    def wait_tile(buffer, place):
        pltpu.make_async_copy(
            panel.at[buffer, place], panel.at[buffer, place], tile_recv.at[buffer, place]
        ).wait()

    x_up, x_down, x_far = (x + 1) % 4, (x + 3) % 4, (x + 2) % 4
    y_up, y_down, y_far = (y + 1) % 4, (y + 3) % 4, (y + 2) % 4

    def gather_start(buffer):
        for step in range(1, 8):
            z_step, step_4 = step // 4, step % 4
            tile_copy(
                buffer,
                my_place,
                (x + step_4 * z_lo) % 4,
                (z_lo + z_step) % 2,
                (y + step_4 * (1 - z_lo)) % 4,
            ).start()

    def gather_forward(buffer):
        for step in range(4):
            place_a = place_of(x, 0, (y + step) % 4)
            place_b = place_of((x + step) % 4, 1, y)
            if step == 0:
                pl.when(z_lo == 1)(lambda: wait_tile(buffer, place_a))
            else:
                wait_tile(buffer, place_a)
            tile_copy(buffer, place_a, x_up, z_lo, y).start()
            tile_copy(buffer, place_a, x_down, z_lo, y).start()
            if step == 0:
                pl.when(z_lo == 0)(lambda: wait_tile(buffer, place_b))
            else:
                wait_tile(buffer, place_b)
            tile_copy(buffer, place_b, x, z_lo, y_up).start()
            tile_copy(buffer, place_b, x, z_lo, y_down).start()
        multiply(x, True)(buffer)
        multiply(4 + y, False)(buffer)
        for step in range(4):
            row_a = (y + step) % 4
            row_b = (x + step) % 4
            up_a, down_a = place_of(x_down, 0, row_a), place_of(x_up, 0, row_a)
            up_b, down_b = place_of(row_b, 1, y_down), place_of(row_b, 1, y_up)
            for place in (up_a, down_a, up_b, down_b):
                wait_tile(buffer, place)
            even_a = row_a % 2 == 0
            tile_copy(
                buffer, jnp.where(even_a, up_a, down_a), jnp.where(even_a, x_up, x_down), z_lo, y
            ).start()
            even_b = row_b % 2 == 0
            tile_copy(
                buffer, jnp.where(even_b, up_b, down_b), x, z_lo, jnp.where(even_b, y_up, y_down)
            ).start()
        multiply(x_down, False)(buffer)
        multiply(x_up, False)(buffer)
        multiply(4 + y_down, False)(buffer)
        multiply(4 + y_up, False)(buffer)
        for step in range(4):
            wait_tile(buffer, place_of(x_far, 0, (y + step) % 4))
            wait_tile(buffer, place_of((x + step) % 4, 1, y_far))

    def core_copy(buffer, part):
        return pltpu.make_async_remote_copy(
            src_ref=partial.at[part * 2 + 1 - core],
            dst_ref=from_core.at[buffer, part],
            send_sem=core_send.at[part],
            recv_sem=core_recv.at[buffer, part],
            device_id={"row": r, "col": z_hi * 2 + 1 - core},
            device_id_type=MESH,
        )

    def z_copy(buffer, step):
        to = (z_hi + step) % 4
        return pltpu.make_async_remote_copy(
            src_ref=combined.at[step - 1],
            dst_ref=from_z.at[buffer, step - 1],
            send_sem=z_send.at[step - 1],
            recv_sem=z_recv.at[buffer, step - 1],
            device_id={"row": r, "col": to * 2 + core},
            device_id_type=MESH,
        )

    def reduce_level(level, buffer, out):
        for part in range(4):
            core_copy(buffer, part).start()
        for step in (2, 1, 3):
            to = (z_hi + step) % 4
            core_copy(buffer, to).wait_recv()
            combined[step - 1] = partial[to * 2 + core] + from_core[buffer, to]
            z_copy(buffer, step).start()
        core_copy(buffer, z_hi).wait_recv()
        mine = partial[z_hi * 2 + core] + from_core[buffer, z_hi]
        for step in (1, 3, 2):
            z_copy(buffer, step).wait_recv()
            mine = mine + from_z[buffer, step - 1]
        raw = jnp.where(depth_ref[...] >= level, mine, 0.0)
        paths[level - 1] = raw
        squares[pl.ds(level - 1, 1), :] = jnp.sum(raw * raw, axis=0, keepdims=True)
        if out is not None:
            panel[out, my_place] = (raw * SHRINK).astype(jnp.bfloat16)

    def drain(buffer):
        for part in range(4):
            core_copy(buffer, part).wait_send()
        for step in (1, 2, 3):
            z_copy(buffer, step).wait_send()

    squares[...] = jnp.zeros_like(squares)

    @pl.loop(0, SRCS)
    def _(row):
        place = place_of(row // 8, (row // 4) % 2, row % 4)
        vertex = (row * N_COL + c) * TILE + lax.broadcasted_iota(jnp.int32, (TILE, PANEL), 0)
        panel[0, place] = (vertex == ids_ref[...]).astype(jnp.float32).astype(jnp.bfloat16)

    multiply(0, True)(0)

    @pl.loop(1, 8)
    def _(chunk):
        multiply(chunk, False)(0)

    pl.semaphore_wait(barrier, N_ROW + N_COL - 2)
    reduce_level(1, 1, 1)

    @pl.loop(2, LEVELS + 1)
    def _(level):
        buffer = (level + 1) % 2
        gather_start(buffer)
        drain(0)
        gather_forward(buffer)
        multiply(x_far, False)(buffer)
        multiply(4 + y_far, False)(buffer)
        sent = panel.at[buffer, pl.ds(0, SRCS - 1)]
        pltpu.make_async_copy(sent, sent, tile_send).wait()
        reduce_level(level, 1 - buffer, 1 - buffer)

    drain(0)

    def col_copy(to):
        return pltpu.make_async_remote_copy(
            src_ref=squares,
            dst_ref=squares_col.at[c],
            send_sem=col_send,
            recv_sem=col_recv.at[c],
            device_id={"row": r, "col": to},
            device_id_type=MESH,
        )

    def row_copy(to):
        return pltpu.make_async_remote_copy(
            src_ref=squares,
            dst_ref=squares_row.at[r],
            send_sem=row_send,
            recv_sem=row_recv.at[r],
            device_id={"row": to, "col": c},
            device_id_type=MESH,
        )

    @pl.loop(1, N_COL)
    def _(step):
        col_copy((c + step) % N_COL).start()

    squares_col[c] = squares[...]

    @pl.loop(1, N_COL)
    def _(step):
        source = (c + step) % N_COL
        pltpu.make_async_copy(squares_col.at[source], squares_col.at[source], col_recv.at[source]).wait()

    sent_col = squares_col.at[pl.ds(0, N_COL - 1)]
    pltpu.make_async_copy(sent_col, sent_col, col_send).wait()
    squares[...] = jnp.sum(squares_col[...], axis=0)

    @pl.loop(1, N_ROW)
    def _(step):
        row_copy((r + step) % N_ROW).start()

    squares_row[r] = squares[...]

    @pl.loop(1, N_ROW)
    def _(step):
        source = (r + step) % N_ROW
        pltpu.make_async_copy(squares_row.at[source], squares_row.at[source], row_recv.at[source]).wait()

    sent_row = squares_row.at[pl.ds(0, N_ROW - 1)]
    pltpu.make_async_copy(sent_row, sent_row, row_send).wait()
    totals = jnp.sum(squares_row[...], axis=0)

    position = r * N_COL + c
    vertex = position * TILE + lax.broadcasted_iota(jnp.int32, (TILE, PANEL), 0)
    sums = (vertex == ids_ref[...]).astype(jnp.float32)
    kappa = jnp.ones((1, PANEL), jnp.float32)
    for level in range(LEVELS):
        mean_square = totals[level : level + 1] / VERTICES / kappa / kappa + EPSILON
        scale = kappa * jnp.sqrt(mean_square)
        sums = sums + paths[level] * (1.0 / scale)
        logs_ref[level : level + 1, :] = 0.5 * jnp.log(mean_square)
        kappa = scale * SHRINK
    sums_ref[...] = sums


def local(adj_tiles, tile_rows, tile_cols, tile_count, tile_depth, source_ids):
    smem = pl.BlockSpec(memory_space=pltpu.SMEM)
    vmem = pl.BlockSpec(memory_space=pltpu.VMEM)
    dense = pl.pallas_call(
        densify,
        out_shape=jax.ShapeDtypeStruct((DESTS * TILE, SRCS * TILE), jnp.bfloat16),
        in_specs=[smem, smem, smem, pl.BlockSpec(memory_space=pl.ANY)],
        out_specs=vmem,
        scratch_shapes=[
            pltpu.VMEM((KMAX, TILE, TILE), jnp.bfloat16),
            pltpu.SemaphoreType.DMA((LOADS,)),
        ],
        compiler_params=pltpu.CompilerParams(vmem_limit_bytes=24 * 2**20),
        name="densify",
    )(tile_count[0], tile_rows[0, 0], tile_cols[0, 0], adj_tiles[0, 0])
    return pl.pallas_call(
        levels_kernel,
        out_shape=(
            jax.ShapeDtypeStruct((TILE, PANEL), jnp.float32),
            jax.ShapeDtypeStruct((LEVELS, PANEL), jnp.float32),
        ),
        in_specs=[vmem, vmem, vmem],
        out_specs=(vmem, vmem),
        scratch_shapes=[
            pltpu.VMEM((2, SRCS, TILE, PANEL), jnp.bfloat16),
            pltpu.VMEM((DESTS, TILE, PANEL), jnp.float32),
            pltpu.VMEM((2, 4, TILE, PANEL), jnp.float32),
            pltpu.VMEM((3, TILE, PANEL), jnp.float32),
            pltpu.VMEM((2, 3, TILE, PANEL), jnp.float32),
            pltpu.VMEM((LEVELS, TILE, PANEL), jnp.float32),
            pltpu.VMEM((8, PANEL), jnp.float32),
            pltpu.VMEM((N_COL, 8, PANEL), jnp.float32),
            pltpu.VMEM((N_ROW, 8, PANEL), jnp.float32),
            pltpu.SemaphoreType.DMA,
            pltpu.SemaphoreType.DMA((2, SRCS)),
            pltpu.SemaphoreType.DMA((4,)),
            pltpu.SemaphoreType.DMA((2, 4)),
            pltpu.SemaphoreType.DMA((3,)),
            pltpu.SemaphoreType.DMA((2, 3)),
            pltpu.SemaphoreType.DMA,
            pltpu.SemaphoreType.DMA((N_COL,)),
            pltpu.SemaphoreType.DMA,
            pltpu.SemaphoreType.DMA((N_ROW,)),
        ],
        compiler_params=pltpu.CompilerParams(
            collective_id=0, has_side_effects=True, vmem_limit_bytes=32 * 2**20
        ),
        name="levels",
    )(dense, tile_depth, source_ids.reshape(1, PANEL))


def solution(mesh):
    in_specs = (
        P("row", "col", None, None, None),
        P("row", "col", None),
        P("row", "col", None),
        P("row", "col"),
        P(("row", "col"), None),
        P(),
    )
    out_specs = (P(("row", "col"), None), P())
    return jax.shard_map(local, mesh=mesh, in_specs=in_specs, out_specs=out_specs, check_vma=False)
```

time: 758 us -> 159 us (0.21); the launches traced: 750 us -> 159 us
  blocking collectives: 452 us -> 0 us
  Pallas kernels: 0 us -> 153 us
  waiting for transfers between devices: 106 us -> 0 us
  starting transfers between devices: 76.4 us -> 0 us
  other arithmetic: 65.2 us -> 0 us
  matrix products: 25.5 us -> 0 us
  local copies, waits for them, and re-layouts: 21.3 us -> 4.72 us
    all_to_all x5 -> x0, blocking collectives: 234 us -> none  [sent_and_summed(): parts = lax.all_to_all(cut_along(shard, dim, count), axis, 0, 0, tiled=True)]
    psum x30 -> x0, blocking collectives: 219 us -> none  [one_axis_at_a_time(): return functools.reduce(lax.psum, axes, shard)]
    pallas_call x0 -> x2, Pallas kernels: none -> 153 us  [the longest x1 150 us: local(): pl.pallas_call(levels_kernel, out_shape=(jax.ShapeDtypeStruct((TILE, PANE...]
    all_to_all x7 -> x0, waiting for transfers between devices: 106 us -> none  [the longest x6 93.4 us: copy_for_each(): return lax.all_to_all(copies, axis, split_axis=0, concat_axis=0, tiled=True)]
    all_to_all x7 -> x0, starting transfers between devices: 76.4 us -> none  [the longest x1 47 us: sent_and_summed(): parts = lax.all_to_all(cut_along(shard, dim, count), axis, 0, 0, tiled=True)]
    scatter-add x18 -> x0, other arithmetic: 34.1 us -> none  [one_turn(): summed.at[part_rows]]
    dot_general x18 -> x0, matrix products: 25.5 us -> none  [one_turn(): jnp.einsum('gij,gjs->gis', part_blocks, picked, preferred_element_type=jn...]
    and x18 -> x0, other arithmetic: 15.1 us -> none  [one_turn(): picked = jnp.take(sources, local_cols, axis=0)]
  transfers between devices with their start and end apart: 7 -> 0, of which waited for: 7 -> 0; matrix products, arithmetic and copies ran while one was open for 0% -> 0% of each run, Pallas kernels for 0% -> 0%
where the time goes in v1:
time: 159 us
  Pallas kernels  153 us (96%)
  local copies, waits for them, and re-layouts  4.72 us (3%)
    pallas_call x1, Pallas kernels, local(): pl.pallas_call(levels_kernel, out_shape=(jax.ShapeDtypeStruct((TILE, PANE...  150 us
    unnamed x12, local copies, waits for them, and re-layouts  4.72 us

profile of v1, /device:TPU:1, one launch (start us, length us, event | category | flops | bytes accessed | tf_op | source)
XLA Modules:
  0.0 159.0 jit_solution(2650002319903525694)
XLA Ops:
  0.6 0.0 copy-start.4
  0.6 0.0 copy-start.3
  1.3 0.0 copy-start
  1.3 2.2 %copy-done = bf16[1,1,128,128,128]{4,3,2,1,0:T(8,128)(2,1)S(1)} copy-done((bf16[1,1,128,128,128]{4,3,2,1,0:T(8,128)(2,1)S(1)}, bf16[1,1,128,128,128]{4,3,2,1,0:T(8,128)(2,1)}, u32[]{:S(2)}) %copy-start) | copy-done | bytes 4194328
  3.5 0.0 copy-start.1
  3.5 0.7 copy-done.1
  4.2 0.0 copy-start.2
  4.2 0.7 copy-done.2
  4.8 3.2 %densify.1.dense = bf16[1024,4096]{1,0:T(8,128)(2,1)S(1)} custom-call(s32[1]{0:T(128)} %bitcast.5.count_ref, s32[128]{0:T(128)S(1)} %bitcast.7, s32[128]{0:T(128)S(1)} %bitcast.8, bf16[128,128,128]{2,1,0:T(8,128)(2,1)S(1)} %bitcast.6), custom_call_target="tpu_custom_call" | custom-call | tf_op jit(solution)/shard_map/densify/pallas_call | solution.py:337
  8.0 0.0 copy-done.4
  8.0 0.0 copy-done.3
  8.0 149.8 %levels.1 = (f32[128,128]{1,0:T(8,128)S(1)}, f32[6,128]{1,0:T(8,128)S(1)}) custom-call(bf16[1024,4096]{1,0:T(8,128)(2,1)S(1)} %densify.1.dense, s32[1,128]{1,0:T(1,128)S(1)} %copy-done.3, s32[1,128]{1,0:T(1,128)S(1)} %bitcast.9), custom_call_target="tpu_custom_call" | custom-call | tf_op jit(solution)/shard_map/levels/pallas_call | solution.py:349
  157.8 0.6 copy.11
  158.4 0.6 copy.12
Async XLA Ops:
  0.6 7.4 %copy-start.4 = (s32[128]{0:T(128)S(1)}, s32[128]{0:T(128)}, u32[]{:S(2)}) copy-start(s32[128]{0:T(128)} %param.11) | copy-start | bytes 1540
  0.6 7.4 %copy-start.3 = (s32[1,128]{1,0:T(1,128)S(1)}, s32[1,128]{1,0:T(1,128)}, u32[]{:S(2)}) copy-start(s32[1,128]{1,0:T(1,128)} %depth_ref.1) | copy-start | bytes 1540
  1.3 2.2 %copy-start = (bf16[1,1,128,128,128]{4,3,2,1,0:T(8,128)(2,1)S(1)}, bf16[1,1,128,128,128]{4,3,2,1,0:T(8,128)(2,1)}, u32[]{:S(2)}) copy-start(bf16[1,1,128,128,128]{4,3,2,1,0:T(8,128)(2,1)} %param.6) | copy-start | bytes 12582916
  3.5 0.7 copy-start.1
  4.2 0.7 copy-start.2

commit v2 on v1

v2 whole, which is shorter than its diff:
```python
import jax
import jax.numpy as jnp
from jax import lax
from jax.experimental import pallas as pl
from jax.experimental.pallas import tpu as pltpu
from jax.sharding import PartitionSpec as P

MESH = pl.DeviceIdType.MESH
TILE = 128
HALF = 64
PANEL = 128
LEVELS = 6
KMAX = 128
DESTS = 8
SRCS = 32
N_ROW = 32
N_COL = 8
VERTICES = 32768
EPSILON = 1e-06
SHRINK_BITS = 10
SHRINK = 2.0**-SHRINK_BITS
GROWTH_BITS = 17
CODES = 65000.0
ZERO_CODE = -32768
LOADS = 8
LOAD_SLOTS = KMAX // LOADS
BLOCK = 256
OTHER, OWN = 0, 2


def place_of(x, z_lo, y):
    return (x * 4 + y) * 2 + z_lo


def row_of(x, z_lo, y):
    return x * 8 + z_lo * 4 + y


def densify(count_hbm, rows_hbm, cols_hbm, tiles_hbm, dense_ref, count_ref, rows_ref, cols_ref, tiles, small_sem, load_sem):
    core = lax.axis_index("col") % 2

    def load(part):
        slots = pl.ds(part * LOAD_SLOTS, LOAD_SLOTS)
        return pltpu.make_async_copy(tiles_hbm.at[0, 0, slots], tiles.at[slots], load_sem.at[part])

    small = (
        pltpu.make_async_copy(count_hbm, count_ref, small_sem.at[0]),
        pltpu.make_async_copy(rows_hbm, rows_ref, small_sem.at[1]),
        pltpu.make_async_copy(cols_hbm, cols_ref, small_sem.at[2]),
    )
    for copy in small:
        copy.start()
    for part in range(LOADS):
        load(part).start()

    @pl.loop(0, DESTS * TILE // 16)
    def _(block):
        rows = pl.ds(pl.multiple_of(block * 16, 16), 16)
        dense_ref[rows, :] = jnp.zeros((16, SRCS * TILE), jnp.bfloat16)

    for copy in small:
        copy.wait()
    count = count_ref[0, 0]
    for part in range(LOADS):
        load(part).wait()

        @pl.loop(part * LOAD_SLOTS, jnp.minimum(count, (part + 1) * LOAD_SLOTS))
        def _(slot):
            dest = rows_ref[0, 0, slot]
            row = cols_ref[0, 0, slot]
            place = place_of(row // 8, (row // 4) % 2, row % 4)
            block = jnp.where(dest % 2 == core, OWN, OTHER)
            columns = pl.ds(pl.multiple_of(place * TILE, TILE), TILE)
            for half in range(2):
                start = (block + half) * BLOCK + (dest // 2) * HALF
                rows = pl.ds(pl.multiple_of(start, HALF), HALF)
                dense_ref[rows, columns] = (
                    dense_ref[rows, columns] + tiles[slot, half * HALF : (half + 1) * HALF]
                )


def levels_kernel(
    dense,
    depth_ref,
    ids_ref,
    sums_ref,
    logs_ref,
    panel,
    partial,
    from_core,
    codes,
    from_z,
    paths,
    early,
    early_z,
    early_xy,
    last,
    last_z,
    last_xy,
    tile_send,
    tile_recv,
    core_send,
    core_recv,
    z_send,
    z_recv,
    norm_send,
    norm_recv,
):
    r = lax.axis_index("row")
    c = lax.axis_index("col")
    x, z_lo, y = r // 8, (r // 4) % 2, r % 4
    z_hi, core = c // 2, c % 2
    my_place = place_of(x, z_lo, y)

    barrier = pltpu.get_barrier_semaphore()

    @pl.loop(1, N_ROW)
    def _(step):
        pl.semaphore_signal(
            barrier, inc=1, device_id={"row": (r + step) % N_ROW, "col": c}, device_id_type=MESH
        )

    @pl.loop(1, N_COL)
    def _(step):
        to = (c + step) % N_COL
        pl.semaphore_signal(barrier, inc=1, device_id={"row": r, "col": to}, device_id_type=MESH)
        pl.semaphore_signal(
            barrier, inc=1, device_id={"row": row_of(x, 1 - z_lo, y), "col": to}, device_id_type=MESH
        )

    def product(buffer, chunks, block):
        rows = slice(block * BLOCK, (block + 1) * BLOCK)
        total = None
        for at_x, at_y in chunks:
            index = at_x * 4 + at_y
            columns = pl.ds(pl.multiple_of(index * 2 * TILE, 2 * TILE), 2 * TILE)
            source = panel[buffer, pl.ds(index * 2, 2)].reshape(2 * TILE, PANEL)
            term = jnp.dot(dense[rows, columns], source, preferred_element_type=jnp.float32)
            total = term if total is None else total + term
        return total

    def half_of(buffer, place, half):
        return panel.at[buffer, place, pl.ds(half * HALF, HALF)]

    def tile_copy(buffer, place, half, to_x, to_z, to_y):
        return pltpu.make_async_remote_copy(
            src_ref=half_of(buffer, place, half),
            dst_ref=half_of(buffer, place, half),
            send_sem=tile_send,
            recv_sem=tile_recv.at[buffer, half, place],
            device_id={"row": row_of(to_x, to_z, to_y), "col": c},
            device_id_type=MESH,
        )

    def wait_tile(buffer, place, half):
        ref = half_of(buffer, place, half)
        pltpu.make_async_copy(ref, ref, tile_recv.at[buffer, half, place]).wait()

    def at(half, along, across, z):
        ahead, side = ((x, y), (y, x))[half]
        ahead, side = (ahead + along) % 4, (side + across) % 4
        return (ahead, (z_lo + z) % 2, side) if half == 0 else (side, (z_lo + z) % 2, ahead)

    def plane_start(buffer, half):
        for along in (1, 3):
            tile_copy(buffer, my_place, half, *at(half, along, 0, 0)).start()
        for across, z in ((2, 1), (2, 0), (1, 1), (3, 1), (1, 0), (3, 0), (0, 1)):
            tile_copy(buffer, my_place, half, *at(half, 0, across, z)).start()

    def forward_plane(buffer, across, z):
        for half in range(2):
            place = place_of(*at(half, 0, across, z))
            wait_tile(buffer, place, half)
            for along in (1, 3):
                tile_copy(buffer, place, half, *at(half, along, 0, 0)).start()

    def forward_ring(buffer, across, z):
        for half in range(2):
            below = place_of(*at(half, 3, across, z))
            above = place_of(*at(half, 1, across, z))
            wait_tile(buffer, below, half)
            wait_tile(buffer, above, half)
            side = ((y, x)[half] + across) % 2
            x_up, _, y_up = at(half, 1, 0, 0)
            x_down, _, y_down = at(half, 3, 0, 0)
            even = side == 0
            tile_copy(
                buffer,
                jnp.where(even, below, above),
                half,
                jnp.where(even, x_up, x_down),
                z_lo,
                jnp.where(even, y_up, y_down),
            ).start()

    def wait_far(buffer, half, across):
        for z in range(2):
            wait_tile(buffer, place_of(*at(half, 2, across, z)), half)

    def spot(step_x, step_y):
        return (x + step_x) % 4, (y + step_y) % 4

    def gather(buffer, wait_sends):
        with jax.named_scope("fwd_plane"):
            forward_plane(buffer, 0, 1)
            forward_ring(buffer, 0, 0)
            for across, z in ((1, 0), (3, 0), (1, 1), (3, 1), (2, 0), (2, 1)):
                forward_plane(buffer, across, z)
        with jax.named_scope("fwd_ring"):
            for across, z in ((0, 1), (1, 0), (3, 0), (1, 1), (3, 1), (2, 0), (2, 1)):
                forward_ring(buffer, across, z)
        with jax.named_scope("mm_near"):
            wait_sends()
            near = [spot(i, j) for i in (0, 1, 3) for j in (0, 1, 3)]
            for block in range(4):
                partial[block] = product(buffer, near, block)
        with jax.named_scope("far_one"):
            for across in (0, 1):
                for half in range(2):
                    wait_far(buffer, half, across)
        with jax.named_scope("mm_one"):
            chunks = [spot(2, 0), spot(0, 2), spot(2, 1), spot(1, 2)]
            for block in range(4):
                partial[block] += product(buffer, chunks, block)
        with jax.named_scope("far_two"):
            for across in (3, 2):
                for half in range(2):
                    wait_far(buffer, half, across)
        return [spot(2, 3), spot(3, 2), spot(2, 2)]

    def core_copy(buffer, half):
        return pltpu.make_async_remote_copy(
            src_ref=partial.at[OTHER + half],
            dst_ref=from_core.at[buffer, half],
            send_sem=core_send.at[half],
            recv_sem=core_recv.at[buffer, half],
            device_id={"row": r, "col": z_hi * 2 + 1 - core},
            device_id_type=MESH,
        )

    def z_copy(buffer, half, step):
        return pltpu.make_async_remote_copy(
            src_ref=codes.at[half, step - 1],
            dst_ref=from_z.at[buffer, half, step - 1],
            send_sem=z_send.at[half, step - 1],
            recv_sem=z_recv.at[buffer, half, step - 1],
            device_id={"row": r, "col": ((z_hi + step) % 4) * 2 + core},
            device_id_type=MESH,
        )

    def code_scale(level):
        before = (jnp.zeros((1, PANEL), jnp.int32) + (level - 1)).astype(jnp.float32)
        steps = CODES / (GROWTH_BITS * (before + 1.0) + 0.5)
        middle = 0.5 * (GROWTH_BITS + (GROWTH_BITS - 2 * SHRINK_BITS) * before)
        return steps, middle

    def both_cores(buffer, half, part):
        rows = pl.ds(pl.multiple_of(part * HALF, HALF), HALF)
        return partial[OWN + half, rows] + from_core[buffer, half, rows]

    def combine(level, buffer, half):
        core_copy(buffer, half).wait_recv()
        steps, middle = code_scale(level)
        for step in (2, 1, 3):
            value = both_cores(buffer, half, (z_hi + step) % 4)
            code = jnp.round((jnp.log2(jnp.maximum(value, 2.0**-60)) - middle) * steps).astype(jnp.int32)
            codes[half, step - 1] = jnp.where(value > 0.0, code, ZERO_CODE).astype(jnp.int16)
            z_copy(buffer, half, step).start()

    def finish(level, buffer, half):
        steps, middle = code_scale(level)
        mine = both_cores(buffer, half, z_hi)
        for step in (1, 3, 2):
            z_copy(buffer, half, step).wait_recv()
            code = from_z[buffer, half, step - 1].astype(jnp.int32)
            value = jnp.exp2(code.astype(jnp.float32) * (1.0 / steps) + middle)
            mine = mine + jnp.where(code == ZERO_CODE, 0.0, value)
        raw = jnp.where(depth_ref[...] >= level, mine, 0.0)
        paths[level - 1, half * HALF : (half + 1) * HALF] = raw
        return raw

    def wait_sends():
        for half in range(2):
            core_copy(0, half).wait_send()
            for step in (1, 2, 3):
                z_copy(0, half, step).wait_send()

    def wait_tile_sends(buffer):
        sent = panel.at[buffer, pl.ds(0, SRCS - 1)]
        pltpu.make_async_copy(sent, sent, tile_send).wait()

    def reduce_level(level, buffer, out, block_product, drain, keep):
        with jax.named_scope("mm_last"):
            for half in range(2):
                partial[OTHER + half] = block_product(OTHER + half)
                core_copy(buffer, half).start()
                if half == 1:
                    with jax.named_scope("combine_0"):
                        combine(level, buffer, 0)
                partial[OWN + half] = block_product(OWN + half)
        with jax.named_scope("combine_1"):
            combine(level, buffer, 1)
            drain()
        squares = jnp.zeros((1, PANEL), jnp.float32)
        for half in range(2):
            with jax.named_scope("finish_%d" % half):
                raw = finish(level, buffer, half)
                squares = squares + jnp.sum(raw * raw, axis=0, keepdims=True)
                if out is not None:
                    panel[out, my_place, half * HALF : (half + 1) * HALF] = (raw * SHRINK).astype(jnp.bfloat16)
                    plane_start(out, half)
        keep(squares)

    mine_z = z_lo * N_COL + c
    mine_xy = x * 4 + y

    def z_peer(step):
        index = (mine_z + step) % 16
        return index, {"row": row_of(x, index // 8, y), "col": index % 8}

    def xy_peer(step):
        index = (mine_xy + step) % 16
        return index, {"row": row_of(index // 4, z_lo, index % 4), "col": c}

    def norm_start(which, source, slots, peer, mine):
        slots[mine] = source[...]

        @pl.loop(1, 16)
        def _(step):
            pltpu.make_async_remote_copy(
                src_ref=source,
                dst_ref=slots.at[mine],
                send_sem=norm_send.at[which],
                recv_sem=norm_recv.at[which, mine],
                device_id=peer(step)[1],
                device_id_type=MESH,
            ).start()

    def norm_wait(which, slots, peer):
        @pl.loop(1, 16)
        def _(step):
            slot = slots.at[peer(step)[0]]
            pltpu.make_async_copy(slot, slot, norm_recv.at[which, peer(step)[0]]).wait()

        sent = slots.at[pl.ds(0, 15)]
        pltpu.make_async_copy(sent, sent, norm_send.at[which]).wait()
        return jnp.sum(slots[...], axis=0)

    with jax.named_scope("onehot"):
        early[...] = jnp.zeros_like(early)

        @pl.loop(0, SRCS)
        def _(row):
            place = place_of(row // 8, (row // 4) % 2, row % 4)
            vertex = (row * N_COL + c) * TILE + lax.broadcasted_iota(jnp.int32, (TILE, PANEL), 0)
            panel[0, place] = (vertex == ids_ref[...]).astype(jnp.float32).astype(jnp.bfloat16)

    def first_product(block):
        partial[block] = product(0, [(0, j) for j in range(4)], block)

        @pl.loop(1, 3)
        def _(at_x):
            partial[block] += product(0, [(at_x, j) for j in range(4)], block)

        total = partial[block] + product(0, [(3, j) for j in range(4)], block)
        if block == OTHER:
            with jax.named_scope("barrier"):
                pl.semaphore_wait(barrier, N_ROW - 1 + 2 * (N_COL - 1))
        return total

    def keep_early(level):
        def keep(squares):
            early[pl.ds(level - 1, 1), :] = squares

        return keep

    reduce_level(1, 1, 1, first_product, lambda: None, keep_early(1))

    @pl.loop(2, LEVELS)
    def _(level):
        buffer = (level + 1) % 2
        chunks = gather(buffer, wait_sends)
        reduce_level(
            level,
            1 - buffer,
            1 - buffer,
            lambda block: partial[block] + product(buffer, chunks, block),
            lambda: wait_tile_sends(buffer),
            keep_early(level),
        )

    norm_start(0, early, early_z, z_peer, mine_z)
    buffer = (LEVELS + 1) % 2

    def middle_of_last():
        wait_sends()
        early[...] = norm_wait(0, early_z, z_peer)
        norm_start(1, early, early_xy, xy_peer, mine_xy)

    chunks = gather(buffer, middle_of_last)

    def keep_last(squares):
        last[...] = squares

    reduce_level(
        LEVELS,
        1 - buffer,
        None,
        lambda block: partial[block] + product(buffer, chunks, block),
        lambda: wait_tile_sends(buffer),
        keep_last,
    )

    with jax.named_scope("norm_z"):
        norm_start(2, last, last_z, z_peer, mine_z)
        wait_sends()
        totals = norm_wait(1, early_xy, xy_peer)
        last[...] = norm_wait(2, last_z, z_peer)
    with jax.named_scope("norm_xy"):
        norm_start(3, last, last_xy, xy_peer, mine_xy)
        last_total = norm_wait(3, last_xy, xy_peer)

    with jax.named_scope("outputs"):
        vertex = (r * N_COL + c) * TILE + lax.broadcasted_iota(jnp.int32, (TILE, PANEL), 0)
        sums = (vertex == ids_ref[...]).astype(jnp.float32)
        kappa = jnp.ones((1, PANEL), jnp.float32)
        for level in range(LEVELS):
            total = totals[level : level + 1] if level < LEVELS - 1 else last_total
            mean_square = total / VERTICES / kappa / kappa + EPSILON
            scale = kappa * jnp.sqrt(mean_square)
            sums = sums + paths[level] * (1.0 / scale)
            logs_ref[level : level + 1, :] = 0.5 * jnp.log(mean_square)
            kappa = scale * SHRINK
        sums_ref[...] = sums


def local(adj_tiles, tile_rows, tile_cols, tile_count, tile_depth, source_ids):
    hbm = pl.BlockSpec(memory_space=pltpu.HBM)
    vmem = pl.BlockSpec(memory_space=pltpu.VMEM)
    dense = pl.pallas_call(
        densify,
        out_shape=jax.ShapeDtypeStruct((DESTS * TILE, SRCS * TILE), jnp.bfloat16),
        in_specs=[hbm, hbm, hbm, hbm],
        out_specs=vmem,
        scratch_shapes=[
            pltpu.SMEM((1, 1), jnp.int32),
            pltpu.SMEM((1, 1, KMAX), jnp.int32),
            pltpu.SMEM((1, 1, KMAX), jnp.int32),
            pltpu.VMEM((KMAX, TILE, TILE), jnp.bfloat16),
            pltpu.SemaphoreType.DMA((3,)),
            pltpu.SemaphoreType.DMA((LOADS,)),
        ],
        compiler_params=pltpu.CompilerParams(vmem_limit_bytes=24 * 2**20),
        name="densify",
    )(tile_count, tile_rows, tile_cols, adj_tiles)
    return pl.pallas_call(
        levels_kernel,
        out_shape=(
            jax.ShapeDtypeStruct((TILE, PANEL), jnp.float32),
            jax.ShapeDtypeStruct((LEVELS, PANEL), jnp.float32),
        ),
        in_specs=[vmem, vmem, vmem],
        out_specs=(vmem, vmem),
        scratch_shapes=[
            pltpu.VMEM((2, SRCS, TILE, PANEL), jnp.bfloat16),
            pltpu.VMEM((4, BLOCK, PANEL), jnp.float32),
            pltpu.VMEM((2, 2, BLOCK, PANEL), jnp.float32),
            pltpu.VMEM((2, 3, HALF, PANEL), jnp.int16),
            pltpu.VMEM((2, 2, 3, HALF, PANEL), jnp.int16),
            pltpu.VMEM((LEVELS, TILE, PANEL), jnp.float32),
            pltpu.VMEM((8, PANEL), jnp.float32),
            pltpu.VMEM((16, 8, PANEL), jnp.float32),
            pltpu.VMEM((16, 8, PANEL), jnp.float32),
            pltpu.VMEM((1, PANEL), jnp.float32),
            pltpu.VMEM((16, 1, PANEL), jnp.float32),
            pltpu.VMEM((16, 1, PANEL), jnp.float32),
            pltpu.SemaphoreType.DMA,
            pltpu.SemaphoreType.DMA((2, 2, SRCS)),
            pltpu.SemaphoreType.DMA((2,)),
            pltpu.SemaphoreType.DMA((2, 2)),
            pltpu.SemaphoreType.DMA((2, 3)),
            pltpu.SemaphoreType.DMA((2, 2, 3)),
            pltpu.SemaphoreType.DMA((4,)),
            pltpu.SemaphoreType.DMA((4, 16)),
        ],
        compiler_params=pltpu.CompilerParams(
            collective_id=0, has_side_effects=True, vmem_limit_bytes=32 * 2**20
        ),
        name="levels",
    )(dense, tile_depth, source_ids.reshape(1, PANEL))


def solution(mesh):
    in_specs = (
        P("row", "col", None, None, None),
        P("row", "col", None),
        P("row", "col", None),
        P("row", "col"),
        P(("row", "col"), None),
        P(),
    )
    out_specs = (P(("row", "col"), None), P())
    return jax.shard_map(local, mesh=mesh, in_specs=in_specs, out_specs=out_specs, check_vma=False)
```

time: 159 us -> 140 us (0.88)
  Pallas kernels: 153 us -> 134 us
    pallas_call x1, Pallas kernels: 150 us -> 131 us  [local(): pl.pallas_call(levels_kernel, out_shape=(jax.ShapeDtypeStruct((TILE, PANE...]
where the time goes in v2:
time: 140 us
  Pallas kernels  134 us (96%)
  local copies, waits for them, and re-layouts  4.72 us (3%)
    pallas_call x1, Pallas kernels, local(): pl.pallas_call(levels_kernel, out_shape=(jax.ShapeDtypeStruct((TILE, PANE...  131 us
    unnamed x12, local copies, waits for them, and re-layouts  4.72 us

profile of v2, /device:TPU:1, one launch (start us, length us, event | category | flops | bytes accessed | tf_op | source)
XLA Modules:
  0.0 140.3 jit_solution(5595273125480974418)
XLA Ops:
  0.6 0.0 copy-start.4
  0.6 0.0 copy-start.3
  1.3 0.0 copy-start
  1.3 2.2 %copy-done = bf16[1,1,128,128,128]{4,3,2,1,0:T(8,128)(2,1)S(1)} copy-done((bf16[1,1,128,128,128]{4,3,2,1,0:T(8,128)(2,1)S(1)}, bf16[1,1,128,128,128]{4,3,2,1,0:T(8,128)(2,1)}, u32[]{:S(2)}) %copy-start) | copy-done | bytes 4194328
  3.5 0.0 copy-start.1
  3.5 0.7 copy-done.1
  4.2 0.0 copy-start.2
  4.2 0.7 copy-done.2
  4.8 2.7 %densify.1.dense = bf16[1024,4096]{1,0:T(8,128)(2,1)S(1)} custom-call(s32[1,1]{1,0:T(1,128)S(6)} %copy.10.count_hbm, s32[1,1,128]{2,1,0:T(1,128)S(1)} %copy-done.1, s32[1,1,128]{2,1,0:T(1,128)S(1)} %copy-done.2, bf16[1,1,128,128,128]{4,3,2,1,0:T(8,128)(2,1)S(1)} %copy-done), custom_call_target="tpu_custom_call" | custom-call | tf_op jit(solution)/shard_map/densify/pallas_call | solution.py:440
  7.5 0.0 copy-done.4
  7.5 0.0 copy-done.3
  7.5 131.5 %levels.1 = (f32[128,128]{1,0:T(8,128)S(1)}, f32[6,128]{1,0:T(8,128)S(1)}) custom-call(bf16[1024,4096]{1,0:T(8,128)(2,1)S(1)} %densify.1.dense, s32[1,128]{1,0:T(1,128)S(1)} %copy-done.3, s32[1,128]{1,0:T(1,128)S(1)} %bitcast.1), custom_call_target="tpu_custom_call" | custom-call | tf_op jit(solution)/shard_map/levels/pallas_call | solution.py:456
  139.0 0.6 copy.11
  139.7 0.6 copy.12
Async XLA Ops:
  0.6 6.9 %copy-start.4 = (s32[128]{0:T(128)S(1)}, s32[128]{0:T(128)}, u32[]{:S(2)}) copy-start(s32[128]{0:T(128)} %param.11) | copy-start | bytes 1540
  0.6 6.9 %copy-start.3 = (s32[1,128]{1,0:T(1,128)S(1)}, s32[1,128]{1,0:T(1,128)}, u32[]{:S(2)}) copy-start(s32[1,128]{1,0:T(1,128)} %depth_ref.1) | copy-start | bytes 1540
  1.3 2.2 %copy-start = (bf16[1,1,128,128,128]{4,3,2,1,0:T(8,128)(2,1)S(1)}, bf16[1,1,128,128,128]{4,3,2,1,0:T(8,128)(2,1)}, u32[]{:S(2)}) copy-start(bf16[1,1,128,128,128]{4,3,2,1,0:T(8,128)(2,1)} %tiles_hbm.1) | copy-start | bytes 12582916
  3.5 0.7 copy-start.1
  4.2 0.7 copy-start.2

commit v3 on v2

--- a/solution.py
+++ b/solution.py
@@ -24,8 +24,17 @@
 ZERO_CODE = -32768
 LOADS = 8
 LOAD_SLOTS = KMAX // LOADS
+TRIP = 4
 BLOCK = 256
 OTHER, OWN = 0, 2
+PARTS = ((0, 48), (48, 48), (96, 32))
+PLANE = ((0, 1), (1, 0), (3, 0), (1, 1), (3, 1), (2, 0), (2, 1))
+FLAT = sorted(
+    ((i, j) for i in range(4) for j in range(4) if i or j), key=lambda s: min(s[0], 4 - s[0]) + min(s[1], 4 - s[1])
+)
+NEAR = [(i, j) for i in (0, 1, 3) for j in (0, 1, 3)] + [(2, 0), (0, 2)]
+FAR_ONE = [(2, 1), (1, 2)]
+FAR_TWO = [(2, 3), (3, 2), (2, 2)]
 
 
 def place_of(x, z_lo, y):
@@ -63,20 +72,22 @@
     count = count_ref[0, 0]
     for part in range(LOADS):
         load(part).wait()
-
-        @pl.loop(part * LOAD_SLOTS, jnp.minimum(count, (part + 1) * LOAD_SLOTS))
-        def _(slot):
-            dest = rows_ref[0, 0, slot]
-            row = cols_ref[0, 0, slot]
-            place = place_of(row // 8, (row // 4) % 2, row % 4)
-            block = jnp.where(dest % 2 == core, OWN, OTHER)
-            columns = pl.ds(pl.multiple_of(place * TILE, TILE), TILE)
-            for half in range(2):
-                start = (block + half) * BLOCK + (dest // 2) * HALF
-                rows = pl.ds(pl.multiple_of(start, HALF), HALF)
-                dense_ref[rows, columns] = (
-                    dense_ref[rows, columns] + tiles[slot, half * HALF : (half + 1) * HALF]
-                )
+        first = part * (LOAD_SLOTS // TRIP)
+
+        @pl.loop(first, jnp.minimum((count + TRIP - 1) // TRIP, first + LOAD_SLOTS // TRIP))
+        def _(trip):
+            for inner in range(TRIP):
+                slot = trip * TRIP + inner
+                dest = rows_ref[0, 0, slot]
+                row = cols_ref[0, 0, slot]
+                place = place_of(row // 8, (row // 4) % 2, row % 4)
+                block = jnp.where(dest % 2 == core, OWN, OTHER)
+                columns = pl.ds(pl.multiple_of(place * TILE, TILE), TILE)
+                for half in range(2):
+                    start = (block + half) * BLOCK + (dest // 2) * HALF
+                    rows = pl.ds(pl.multiple_of(start, HALF), HALF)
+                    tile = tiles[slot, half * HALF : (half + 1) * HALF]
+                    dense_ref[rows, columns] += jnp.where(slot < count, tile, jnp.zeros_like(tile))
 
 
 def levels_kernel(
@@ -139,94 +150,90 @@
             total = term if total is None else total + term
         return total
 
-    def half_of(buffer, place, half):
-        return panel.at[buffer, place, pl.ds(half * HALF, HALF)]
-
-    def tile_copy(buffer, place, half, to_x, to_z, to_y):
+    def part_of(buffer, place, part):
+        start, size = PARTS[part]
+        return panel.at[buffer, place, pl.ds(start, size)]
+
+    def tile_copy(buffer, place, part, to_x, to_z, to_y):
         return pltpu.make_async_remote_copy(
-            src_ref=half_of(buffer, place, half),
-            dst_ref=half_of(buffer, place, half),
+            src_ref=part_of(buffer, place, part),
+            dst_ref=part_of(buffer, place, part),
             send_sem=tile_send,
-            recv_sem=tile_recv.at[buffer, half, place],
+            recv_sem=tile_recv.at[buffer, part, place],
             device_id={"row": row_of(to_x, to_z, to_y), "col": c},
             device_id_type=MESH,
         )
 
-    def wait_tile(buffer, place, half):
-        ref = half_of(buffer, place, half)
-        pltpu.make_async_copy(ref, ref, tile_recv.at[buffer, half, place]).wait()
-
-    def at(half, along, across, z):
-        ahead, side = ((x, y), (y, x))[half]
+    def wait_tile(buffer, place, part):
+        ref = part_of(buffer, place, part)
+        pltpu.make_async_copy(ref, ref, tile_recv.at[buffer, part, place]).wait()
+
+    def at(part, along, across, z):
+        ahead, side = ((x, y), (y, x))[part]
         ahead, side = (ahead + along) % 4, (side + across) % 4
-        return (ahead, (z_lo + z) % 2, side) if half == 0 else (side, (z_lo + z) % 2, ahead)
-
-    def plane_start(buffer, half):
-        for along in (1, 3):
-            tile_copy(buffer, my_place, half, *at(half, along, 0, 0)).start()
-        for across, z in ((2, 1), (2, 0), (1, 1), (3, 1), (1, 0), (3, 0), (0, 1)):
-            tile_copy(buffer, my_place, half, *at(half, 0, across, z)).start()
-
-    def forward_plane(buffer, across, z):
-        for half in range(2):
-            place = place_of(*at(half, 0, across, z))
-            wait_tile(buffer, place, half)
-            for along in (1, 3):
-                tile_copy(buffer, place, half, *at(half, along, 0, 0)).start()
-
-    def forward_ring(buffer, across, z):
-        for half in range(2):
-            below = place_of(*at(half, 3, across, z))
-            above = place_of(*at(half, 1, across, z))
-            wait_tile(buffer, below, half)
-            wait_tile(buffer, above, half)
-            side = ((y, x)[half] + across) % 2
-            x_up, _, y_up = at(half, 1, 0, 0)
-            x_down, _, y_down = at(half, 3, 0, 0)
-            even = side == 0
-            tile_copy(
-                buffer,
-                jnp.where(even, below, above),
-                half,
-                jnp.where(even, x_up, x_down),
-                z_lo,
-                jnp.where(even, y_up, y_down),
-            ).start()
-
-    def wait_far(buffer, half, across):
-        for z in range(2):
-            wait_tile(buffer, place_of(*at(half, 2, across, z)), half)
+        return (ahead, (z_lo + z) % 2, side) if part == 0 else (side, (z_lo + z) % 2, ahead)
+
+    def flat(step_x, step_y, z):
+        return (x + step_x) % 4, (z_lo + z) % 2, (y + step_y) % 4
+
+    def send_along(buffer, place, part):
+        for along in (1, 3, 2):
+            tile_copy(buffer, place, part, *at(part, along, 0, 0)).start()
+
+    def start_routed(buffer, part):
+        for across, z in PLANE:
+            tile_copy(buffer, my_place, part, *at(part, 0, across, z)).start()
+        send_along(buffer, my_place, part)
+
+    def start_flat(buffer):
+        tile_copy(buffer, my_place, 2, *flat(0, 0, 1)).start()
+        for step_x, step_y in FLAT:
+            tile_copy(buffer, my_place, 2, *flat(step_x, step_y, 0)).start()
+
+    def gather(buffer, wait_sends):
+        with jax.named_scope("routed"):
+            for across, z in PLANE:
+                for part in range(2):
+                    place = place_of(*at(part, 0, across, z))
+                    wait_tile(buffer, place, part)
+                    send_along(buffer, place, part)
+        with jax.named_scope("flat"):
+            for step_x, step_y in FLAT:
+                place = place_of(*flat(step_x, step_y, 0))
+                wait_tile(buffer, place, 2)
+                tile_copy(buffer, place, 2, *flat(0, 0, 1)).start()
+        with jax.named_scope("wait_near"):
+            for z in range(2):
+                for across in (0, 1, 3):
+                    for along in (1, 3) if across else (1, 3, 2):
+                        for part in range(2):
+                            wait_tile(buffer, place_of(*at(part, along, across, z)), part)
+            for step in NEAR:
+                wait_tile(buffer, place_of(*flat(*step, 1)), 2)
+        with jax.named_scope("mm_near"):
+            wait_sends()
+            chunks = [spot(*step) for step in NEAR]
+            for block in range(4):
+                partial[block] = product(buffer, chunks, block)
+        with jax.named_scope("wait_one"):
+            wait_far(buffer, FAR_ONE)
+        with jax.named_scope("mm_one"):
+            chunks = [spot(*step) for step in FAR_ONE]
+            for block in range(4):
+                partial[block] += product(buffer, chunks, block)
+        with jax.named_scope("wait_two"):
+            wait_far(buffer, FAR_TWO)
+        return [spot(*step) for step in FAR_TWO]
 
     def spot(step_x, step_y):
         return (x + step_x) % 4, (y + step_y) % 4
 
-    def gather(buffer, wait_sends):
-        with jax.named_scope("fwd_plane"):
-            forward_plane(buffer, 0, 1)
-            forward_ring(buffer, 0, 0)
-            for across, z in ((1, 0), (3, 0), (1, 1), (3, 1), (2, 0), (2, 1)):
-                forward_plane(buffer, across, z)
-        with jax.named_scope("fwd_ring"):
-            for across, z in ((0, 1), (1, 0), (3, 0), (1, 1), (3, 1), (2, 0), (2, 1)):
-                forward_ring(buffer, across, z)
-        with jax.named_scope("mm_near"):
-            wait_sends()
-            near = [spot(i, j) for i in (0, 1, 3) for j in (0, 1, 3)]
-            for block in range(4):
-                partial[block] = product(buffer, near, block)
-        with jax.named_scope("far_one"):
-            for across in (0, 1):
-                for half in range(2):
-                    wait_far(buffer, half, across)
-        with jax.named_scope("mm_one"):
-            chunks = [spot(2, 0), spot(0, 2), spot(2, 1), spot(1, 2)]
-            for block in range(4):
-                partial[block] += product(buffer, chunks, block)
-        with jax.named_scope("far_two"):
-            for across in (3, 2):
-                for half in range(2):
-                    wait_far(buffer, half, across)
-        return [spot(2, 3), spot(3, 2), spot(2, 2)]
+    def wait_far(buffer, steps):
+        for step_x, step_y in steps:
+            for z in range(2):
+                wait_tile(buffer, place_of(*at(0, step_x, step_y, z)), 0)
+                wait_tile(buffer, place_of(*at(1, step_y, step_x, z)), 1)
+            wait_tile(buffer, place_of(*flat(step_x, step_y, 1)), 2)
 
     def core_copy(buffer, half):
         return pltpu.make_async_remote_copy(
@@ -308,7 +315,9 @@
                 squares = squares + jnp.sum(raw * raw, axis=0, keepdims=True)
                 if out is not None:
                     panel[out, my_place, half * HALF : (half + 1) * HALF] = (raw * SHRINK).astype(jnp.bfloat16)
-                    plane_start(out, half)
+                    start_routed(out, half)
+                    if half == 1:
+                        start_flat(out)
         keep(squares)
 
     mine_z = z_lo * N_COL + c
@@ -439,7 +448,7 @@
     vmem = pl.BlockSpec(memory_space=pltpu.VMEM)
     dense = pl.pallas_call(
         densify,
-        out_shape=jax.ShapeDtypeStruct((DESTS * TILE, SRCS * TILE), jnp.bfloat16),
+        out_shape=pltpu.VMEM((DESTS * TILE, SRCS * TILE), jnp.bfloat16),
         in_specs=[hbm, hbm, hbm, hbm],
         out_specs=vmem,
         scratch_shapes=[
@@ -450,7 +459,7 @@
             pltpu.SemaphoreType.DMA((3,)),
             pltpu.SemaphoreType.DMA((LOADS,)),
         ],
-        compiler_params=pltpu.CompilerParams(vmem_limit_bytes=24 * 2**20),
+        compiler_params=pltpu.CompilerParams(vmem_limit_bytes=53 * 2**20),
         name="densify",
     )(tile_count, tile_rows, tile_cols, adj_tiles)
     return pl.pallas_call(
@@ -475,7 +484,7 @@
             pltpu.VMEM((16, 1, PANEL), jnp.float32),
             pltpu.VMEM((16, 1, PANEL), jnp.float32),
             pltpu.SemaphoreType.DMA,
-            pltpu.SemaphoreType.DMA((2, 2, SRCS)),
+            pltpu.SemaphoreType.DMA((2, 3, SRCS)),
             pltpu.SemaphoreType.DMA((2,)),
             pltpu.SemaphoreType.DMA((2, 2)),
             pltpu.SemaphoreType.DMA((2, 3)),

time: 140 us -> 129 us (0.921)
  Pallas kernels: 134 us -> 127 us
  local copies, waits for them, and re-layouts: 4.72 us -> 1.23 us
    pallas_call x1, Pallas kernels: 131 us -> 124 us  [local(): pl.pallas_call(levels_kernel, out_shape=(jax.ShapeDtypeStruct((TILE, PANE...]
    unnamed x12 -> x6, local copies, waits for them, and re-layouts: 4.72 us -> 1.23 us
where the time goes in v3:
time: 129 us
  Pallas kernels  127 us (98%)
  between operations  1.34 us (1%)
    pallas_call x1, Pallas kernels, local(): pl.pallas_call(levels_kernel, out_shape=(jax.ShapeDtypeStruct((TILE, PANE...  124 us

profile of v3, /device:TPU:1, one launch (start us, length us, event | category | flops | bytes accessed | tf_op | source)
XLA Modules:
  0.0 129.2 jit_solution(10501335944470303116)
XLA Ops:
  0.6 0.0 copy-start.1
  0.6 0.0 copy-start
  1.3 2.5 %densify.1.dense = bf16[1024,4096]{1,0:T(8,128)(2,1)S(1)} custom-call(s32[1,1]{1,0:T(1,128)S(6)} %copy.10.count_hbm, s32[1,1,128]{2,1,0:T(1,128)} %rows_hbm.1, s32[1,1,128]{2,1,0:T(1,128)} %cols_hbm.1, bf16[1,1,128,128,128]{4,3,2,1,0:T(8,128)(2,1)} %tiles_hbm.1), custom_call_target="tpu_custom_call" | custom-call | tf_op jit(solution)/shard_map/densify/pallas_call | solution.py:449
  3.8 0.0 copy-done.1
  3.8 0.0 copy-done
  3.8 124.2 %levels.1 = (f32[128,128]{1,0:T(8,128)S(1)}, f32[6,128]{1,0:T(8,128)S(1)}) custom-call(bf16[1024,4096]{1,0:T(8,128)(2,1)S(1)} %densify.1.dense, s32[1,128]{1,0:T(1,128)S(1)} %copy-done, s32[1,128]{1,0:T(1,128)S(1)} %bitcast.1), custom_call_target="tpu_custom_call" | custom-call | tf_op jit(solution)/shard_map/levels/pallas_call | solution.py:465
  128.0 0.6 copy.11
  128.6 0.6 copy.12
Async XLA Ops:
  0.6 3.2 %copy-start.1 = (s32[128]{0:T(128)S(1)}, s32[128]{0:T(128)}, u32[]{:S(2)}) copy-start(s32[128]{0:T(128)} %param.11) | copy-start | bytes 1540
  0.6 3.2 %copy-start = (s32[1,128]{1,0:T(1,128)S(1)}, s32[1,128]{1,0:T(1,128)}, u32[]{:S(2)}) copy-start(s32[1,128]{1,0:T(1,128)} %depth_ref.1) | copy-start | bytes 1540

commit v4 on v3

--- a/solution.py
+++ b/solution.py
@@ -25,16 +25,19 @@
 LOADS = 8
 LOAD_SLOTS = KMAX // LOADS
 TRIP = 4
-BLOCK = 256
-OTHER, OWN = 0, 2
+SIDE = 512
+OTHER, OWN = 0, 1
 PARTS = ((0, 48), (48, 48), (96, 32))
 PLANE = ((0, 1), (1, 0), (3, 0), (1, 1), (3, 1), (2, 0), (2, 1))
 FLAT = sorted(
     ((i, j) for i in range(4) for j in range(4) if i or j), key=lambda s: min(s[0], 4 - s[0]) + min(s[1], 4 - s[1])
 )
-NEAR = [(i, j) for i in (0, 1, 3) for j in (0, 1, 3)] + [(2, 0), (0, 2)]
-FAR_ONE = [(2, 1), (1, 2)]
-FAR_TWO = [(2, 3), (3, 2), (2, 2)]
+GROUPS = (
+    ((0, 0), (0, 1), (0, 3), (1, 0), (3, 0)),
+    ((1, 1), (1, 3), (3, 1), (3, 3)),
+    ((2, 0), (0, 2), (2, 1), (1, 2)),
+    ((2, 3), (3, 2), (2, 2)),
+)
 
 
 def place_of(x, z_lo, y):
@@ -62,10 +65,10 @@
     for part in range(LOADS):
         load(part).start()
 
-    @pl.loop(0, DESTS * TILE // 16)
+    @pl.loop(0, SRCS * TILE // 64)
     def _(block):
-        rows = pl.ds(pl.multiple_of(block * 16, 16), 16)
-        dense_ref[rows, :] = jnp.zeros((16, SRCS * TILE), jnp.bfloat16)
+        rows = pl.ds(pl.multiple_of(block * 64, 64), 64)
+        dense_ref[rows, :] = jnp.zeros((64, DESTS * TILE), jnp.bfloat16)
 
     for copy in small:
         copy.wait()
@@ -81,13 +84,11 @@
                 dest = rows_ref[0, 0, slot]
                 row = cols_ref[0, 0, slot]
                 place = place_of(row // 8, (row // 4) % 2, row % 4)
-                block = jnp.where(dest % 2 == core, OWN, OTHER)
-                columns = pl.ds(pl.multiple_of(place * TILE, TILE), TILE)
-                for half in range(2):
-                    start = (block + half) * BLOCK + (dest // 2) * HALF
-                    rows = pl.ds(pl.multiple_of(start, HALF), HALF)
-                    tile = tiles[slot, half * HALF : (half + 1) * HALF]
-                    dense_ref[rows, columns] += jnp.where(slot < count, tile, jnp.zeros_like(tile))
+                side = jnp.where(dest % 2 == core, OWN, OTHER)
+                rows = pl.ds(pl.multiple_of(place * TILE, TILE), TILE)
+                columns = pl.ds(pl.multiple_of(side * SIDE + (dest // 2) * TILE, TILE), TILE)
+                tile = tiles[slot].T
+                dense_ref[rows, columns] += jnp.where(slot < count, tile, jnp.zeros_like(tile))
 
 
 def levels_kernel(
@@ -97,6 +98,7 @@
     sums_ref,
     logs_ref,
     panel,
+    depth,
     partial,
     from_core,
     codes,
@@ -139,14 +141,14 @@
             barrier, inc=1, device_id={"row": row_of(x, 1 - z_lo, y), "col": to}, device_id_type=MESH
         )
 
-    def product(buffer, chunks, block):
-        rows = slice(block * BLOCK, (block + 1) * BLOCK)
+    def product(buffer, chunks, side):
+        columns = slice(side * SIDE, (side + 1) * SIDE)
         total = None
         for at_x, at_y in chunks:
             index = at_x * 4 + at_y
-            columns = pl.ds(pl.multiple_of(index * 2 * TILE, 2 * TILE), 2 * TILE)
-            source = panel[buffer, pl.ds(index * 2, 2)].reshape(2 * TILE, PANEL)
-            term = jnp.dot(dense[rows, columns], source, preferred_element_type=jnp.float32)
+            rows = pl.ds(pl.multiple_of(index * 2 * TILE, 2 * TILE), 2 * TILE)
+            source = jnp.concatenate([panel[buffer, index * 2], panel[buffer, index * 2 + 1]], axis=1)
+            term = jnp.dot(source, dense[rows, columns], preferred_element_type=jnp.float32)
             total = term if total is None else total + term
         return total
 
@@ -202,42 +204,36 @@
                 place = place_of(*flat(step_x, step_y, 0))
                 wait_tile(buffer, place, 2)
                 tile_copy(buffer, place, 2, *flat(0, 0, 1)).start()
-        with jax.named_scope("wait_near"):
-            for z in range(2):
-                for across in (0, 1, 3):
-                    for along in (1, 3) if across else (1, 3, 2):
-                        for part in range(2):
-                            wait_tile(buffer, place_of(*at(part, along, across, z)), part)
-            for step in NEAR:
-                wait_tile(buffer, place_of(*flat(*step, 1)), 2)
-        with jax.named_scope("mm_near"):
-            wait_sends()
-            chunks = [spot(*step) for step in NEAR]
-            for block in range(4):
-                partial[block] = product(buffer, chunks, block)
-        with jax.named_scope("wait_one"):
-            wait_far(buffer, FAR_ONE)
-        with jax.named_scope("mm_one"):
-            chunks = [spot(*step) for step in FAR_ONE]
-            for block in range(4):
-                partial[block] += product(buffer, chunks, block)
-        with jax.named_scope("wait_two"):
-            wait_far(buffer, FAR_TWO)
-        return [spot(*step) for step in FAR_TWO]
+        for number, group in enumerate(GROUPS):
+            with jax.named_scope("wait_group_%d" % number):
+                wait_group(buffer, group)
+                if number == 0:
+                    wait_sends()
+            if number < len(GROUPS) - 1:
+                with jax.named_scope("mm_group_%d" % number):
+                    chunks = [spot(*step) for step in group]
+                    for side in range(2):
+                        if number == 0:
+                            partial[side] = product(buffer, chunks, side)
+                        else:
+                            partial[side] += product(buffer, chunks, side)
+        return [spot(*step) for step in GROUPS[-1]]
 
     def spot(step_x, step_y):
         return (x + step_x) % 4, (y + step_y) % 4
 
-    def wait_far(buffer, steps):
+    def wait_group(buffer, steps):
         for step_x, step_y in steps:
             for z in range(2):
-                wait_tile(buffer, place_of(*at(0, step_x, step_y, z)), 0)
-                wait_tile(buffer, place_of(*at(1, step_y, step_x, z)), 1)
+                if step_x:
+                    wait_tile(buffer, place_of(*at(0, step_x, step_y, z)), 0)
+                if step_y:
+                    wait_tile(buffer, place_of(*at(1, step_y, step_x, z)), 1)
             wait_tile(buffer, place_of(*flat(step_x, step_y, 1)), 2)
 
     def core_copy(buffer, half):
         return pltpu.make_async_remote_copy(
-            src_ref=partial.at[OTHER + half],
+            src_ref=partial.at[OTHER, pl.ds(half * HALF, HALF)],
             dst_ref=from_core.at[buffer, half],
             send_sem=core_send.at[half],
             recv_sem=core_recv.at[buffer, half],
@@ -262,8 +258,8 @@
         return steps, middle
 
     def both_cores(buffer, half, part):
-        rows = pl.ds(pl.multiple_of(part * HALF, HALF), HALF)
-        return partial[OWN + half, rows] + from_core[buffer, half, rows]
+        columns = pl.ds(pl.multiple_of(part * TILE, TILE), TILE)
+        return partial[OWN, half * HALF : (half + 1) * HALF, columns] + from_core[buffer, half, :, columns]
 
     def combine(level, buffer, half):
         core_copy(buffer, half).wait_recv()
@@ -282,8 +278,9 @@
             code = from_z[buffer, half, step - 1].astype(jnp.int32)
             value = jnp.exp2(code.astype(jnp.float32) * (1.0 / steps) + middle)
             mine = mine + jnp.where(code == ZERO_CODE, 0.0, value)
-        raw = jnp.where(depth_ref[...] >= level, mine, 0.0)
-        paths[level - 1, half * HALF : (half + 1) * HALF] = raw
+        rows = slice(half * HALF, (half + 1) * HALF)
+        raw = jnp.where(depth[rows] >= level, mine, 0.0)
+        paths[level - 1, rows] = raw
         return raw
 
     def wait_sends():
@@ -296,29 +293,28 @@
         sent = panel.at[buffer, pl.ds(0, SRCS - 1)]
         pltpu.make_async_copy(sent, sent, tile_send).wait()
 
-    def reduce_level(level, buffer, out, block_product, drain, keep):
+    def reduce_level(level, buffer, out, side_product, drain, keep):
         with jax.named_scope("mm_last"):
+            partial[OTHER] = side_product(OTHER)
             for half in range(2):
-                partial[OTHER + half] = block_product(OTHER + half)
                 core_copy(buffer, half).start()
-                if half == 1:
-                    with jax.named_scope("combine_0"):
-                        combine(level, buffer, 0)
-                partial[OWN + half] = block_product(OWN + half)
-        with jax.named_scope("combine_1"):
-            combine(level, buffer, 1)
+            partial[OWN] = side_product(OWN)
+        with jax.named_scope("combine"):
+            for half in range(2):
+                combine(level, buffer, half)
             drain()
-        squares = jnp.zeros((1, PANEL), jnp.float32)
         for half in range(2):
             with jax.named_scope("finish_%d" % half):
                 raw = finish(level, buffer, half)
-                squares = squares + jnp.sum(raw * raw, axis=0, keepdims=True)
                 if out is not None:
                     panel[out, my_place, half * HALF : (half + 1) * HALF] = (raw * SHRINK).astype(jnp.bfloat16)
                     start_routed(out, half)
                     if half == 1:
                         start_flat(out)
-        keep(squares)
+        with jax.named_scope("squares"):
+            by_vertex = paths[level - 1].T
+            keep(jnp.sum(by_vertex * by_vertex, axis=0, keepdims=True))
+            paths[level - 1] = by_vertex
 
     mine_z = z_lo * N_COL + c
     mine_xy = x * 4 + y
@@ -357,22 +353,24 @@
 
     with jax.named_scope("onehot"):
         early[...] = jnp.zeros_like(early)
+        depth[...] = jnp.broadcast_to(depth_ref[...], (TILE, PANEL)).astype(jnp.float32).T.astype(jnp.int32)
+        ids = jnp.broadcast_to(ids_ref[...], (TILE, PANEL)).astype(jnp.float32).T.astype(jnp.int32)
 
         @pl.loop(0, SRCS)
         def _(row):
             place = place_of(row // 8, (row // 4) % 2, row % 4)
-            vertex = (row * N_COL + c) * TILE + lax.broadcasted_iota(jnp.int32, (TILE, PANEL), 0)
-            panel[0, place] = (vertex == ids_ref[...]).astype(jnp.float32).astype(jnp.bfloat16)
-
-    def first_product(block):
-        partial[block] = product(0, [(0, j) for j in range(4)], block)
+            vertex = (row * N_COL + c) * TILE + lax.broadcasted_iota(jnp.int32, (PANEL, TILE), 1)
+            panel[0, place] = (vertex == ids).astype(jnp.float32).astype(jnp.bfloat16)
+
+    def first_product(side):
+        partial[side] = product(0, [(0, j) for j in range(4)], side)
 
         @pl.loop(1, 3)
         def _(at_x):
-            partial[block] += product(0, [(at_x, j) for j in range(4)], block)
-
-        total = partial[block] + product(0, [(3, j) for j in range(4)], block)
-        if block == OTHER:
+            partial[side] += product(0, [(at_x, j) for j in range(4)], side)
+
+        total = partial[side] + product(0, [(3, j) for j in range(4)], side)
+        if side == OTHER:
             with jax.named_scope("barrier"):
                 pl.semaphore_wait(barrier, N_ROW - 1 + 2 * (N_COL - 1))
         return total
@@ -393,7 +391,7 @@
             level,
             1 - buffer,
             1 - buffer,
-            lambda block: partial[block] + product(buffer, chunks, block),
+            lambda side: partial[side] + product(buffer, chunks, side),
             lambda: wait_tile_sends(buffer),
             keep_early(level),
         )
@@ -415,7 +413,7 @@
         LEVELS,
         1 - buffer,
         None,
-        lambda block: partial[block] + product(buffer, chunks, block),
+        lambda side: partial[side] + product(buffer, chunks, side),
         lambda: wait_tile_sends(buffer),
         keep_last,
     )
@@ -448,7 +446,7 @@
     vmem = pl.BlockSpec(memory_space=pltpu.VMEM)
     dense = pl.pallas_call(
         densify,
-        out_shape=pltpu.VMEM((DESTS * TILE, SRCS * TILE), jnp.bfloat16),
+        out_shape=pltpu.VMEM((SRCS * TILE, DESTS * TILE), jnp.bfloat16),
         in_specs=[hbm, hbm, hbm, hbm],
         out_specs=vmem,
         scratch_shapes=[
@@ -472,8 +470,9 @@
         out_specs=(vmem, vmem),
         scratch_shapes=[
             pltpu.VMEM((2, SRCS, TILE, PANEL), jnp.bfloat16),
-            pltpu.VMEM((4, BLOCK, PANEL), jnp.float32),
-            pltpu.VMEM((2, 2, BLOCK, PANEL), jnp.float32),
+            pltpu.VMEM((PANEL, TILE), jnp.int32),
+            pltpu.VMEM((2, PANEL, SIDE), jnp.float32),
+            pltpu.VMEM((2, 2, HALF, SIDE), jnp.float32),
             pltpu.VMEM((2, 3, HALF, PANEL), jnp.int16),
             pltpu.VMEM((2, 2, 3, HALF, PANEL), jnp.int16),
             pltpu.VMEM((LEVELS, TILE, PANEL), jnp.float32),

time: 129 us -> 122 us (0.946)
  Pallas kernels: 127 us -> 120 us
    pallas_call x1, Pallas kernels: 124 us -> 115 us  [local(): pl.pallas_call(levels_kernel, out_shape=(jax.ShapeDtypeStruct((TILE, PANE...]
    pallas_call x1, Pallas kernels: 2.47 us -> 4.49 us  [local(): pl.pallas_call(densify, out_shape=pltpu.VMEM((SRCS * TILE, DESTS * TILE),...]
where the time goes in v4:
time: 122 us
  Pallas kernels  120 us (98%)
  between operations  1.34 us (1%)
  local copies, waits for them, and re-layouts  1.23 us (1%)
    pallas_call x1, Pallas kernels, local(): pl.pallas_call(levels_kernel, out_shape=(jax.ShapeDtypeStruct((TILE, PANE...  115 us
    pallas_call x1, Pallas kernels, local(): pl.pallas_call(densify, out_shape=pltpu.VMEM((SRCS * TILE, DESTS * TILE),...  4.49 us

profile of v4, /device:TPU:1, one launch (start us, length us, event | category | flops | bytes accessed | tf_op | source)
XLA Modules:
  0.0 122.1 jit_solution(7807538049527415938)
XLA Ops:
  0.6 0.0 copy-start.1
  0.6 0.0 copy-start
  1.3 4.5 %densify.1.dense = bf16[4096,1024]{1,0:T(8,128)(2,1)S(1)} custom-call(s32[1,1]{1,0:T(1,128)S(6)} %copy.10.count_hbm, s32[1,1,128]{2,1,0:T(1,128)} %rows_hbm.1, s32[1,1,128]{2,1,0:T(1,128)} %cols_hbm.1, bf16[1,1,128,128,128]{4,3,2,1,0:T(8,128)(2,1)} %tiles_hbm.1), custom_call_target="tpu_custom_call" | custom-call | tf_op jit(solution)/shard_map/densify/pallas_call | solution.py:447
  5.8 0.0 copy-done.1
  5.8 0.0 copy-done
  5.8 115.0 %levels.1 = (f32[128,128]{1,0:T(8,128)S(1)}, f32[6,128]{1,0:T(8,128)S(1)}) custom-call(bf16[4096,1024]{1,0:T(8,128)(2,1)S(1)} %densify.1.dense, s32[1,128]{1,0:T(1,128)S(1)} %copy-done, s32[1,128]{1,0:T(1,128)S(1)} %bitcast.1), custom_call_target="tpu_custom_call" | custom-call | tf_op jit(solution)/shard_map/levels/pallas_call | solution.py:463
  120.9 0.6 copy.11
  121.5 0.6 copy.12
Async XLA Ops:
  0.6 5.2 %copy-start.1 = (s32[128]{0:T(128)S(1)}, s32[128]{0:T(128)}, u32[]{:S(2)}) copy-start(s32[128]{0:T(128)} %param.11) | copy-start | bytes 1540
  0.6 5.2 %copy-start = (s32[1,128]{1,0:T(1,128)S(1)}, s32[1,128]{1,0:T(1,128)}, u32[]{:S(2)}) copy-start(s32[1,128]{1,0:T(1,128)} %depth_ref.1) | copy-start | bytes 1540

commit v5 on v4

--- a/solution.py
+++ b/solution.py
@@ -24,7 +24,7 @@
 ZERO_CODE = -32768
 LOADS = 8
 LOAD_SLOTS = KMAX // LOADS
-TRIP = 4
+TRIP = 16
 SIDE = 512
 OTHER, OWN = 0, 1
 PARTS = ((0, 48), (48, 48), (96, 32))
@@ -32,6 +32,12 @@
 FLAT = sorted(
     ((i, j) for i in range(4) for j in range(4) if i or j), key=lambda s: min(s[0], 4 - s[0]) + min(s[1], 4 - s[1])
 )
+RELAYS = (
+    *((0, i, z) for i, z in ((0, 1), (1, 0), (3, 0), (1, 1), (3, 1))),
+    *((1, i, z) for i, z in ((0, 1), (1, 0), (3, 0))),
+    *((0, i, z) for i, z in ((2, 0), (2, 1))),
+    *((1, i, z) for i, z in ((1, 1), (3, 1), (2, 0), (2, 1))),
+)
 GROUPS = (
     ((0, 0), (0, 1), (0, 3), (1, 0), (3, 0)),
     ((1, 1), (1, 3), (3, 1), (3, 3)),
@@ -40,8 +46,8 @@
 )
 
 
-def place_of(x, z_lo, y):
-    return (x * 4 + y) * 2 + z_lo
+def place_of(step_x, step_y, step_z):
+    return (step_x % 4 * 4 + step_y % 4) * 2 + step_z % 2
 
 
 def row_of(x, z_lo, y):
@@ -50,6 +56,8 @@
 
 def densify(count_hbm, rows_hbm, cols_hbm, tiles_hbm, dense_ref, count_ref, rows_ref, cols_ref, tiles, small_sem, load_sem):
     core = lax.axis_index("col") % 2
+    r = lax.axis_index("row")
+    x, z_lo, y = r // 8, (r // 4) % 2, r % 4
 
     def load(part):
         slots = pl.ds(part * LOAD_SLOTS, LOAD_SLOTS)
@@ -83,10 +91,11 @@
                 slot = trip * TRIP + inner
                 dest = rows_ref[0, 0, slot]
                 row = cols_ref[0, 0, slot]
-                place = place_of(row // 8, (row // 4) % 2, row % 4)
-                side = jnp.where(dest % 2 == core, OWN, OTHER)
+                steps = (((row >> 3) - x) & 3, (row - y) & 3, ((row >> 2) ^ z_lo) & 1)
+                place = steps[0] * 8 + steps[1] * 2 + steps[2]
+                side = 1 - ((dest ^ core) & 1)
                 rows = pl.ds(pl.multiple_of(place * TILE, TILE), TILE)
-                columns = pl.ds(pl.multiple_of(side * SIDE + (dest // 2) * TILE, TILE), TILE)
+                columns = pl.ds(pl.multiple_of(side * SIDE + (dest >> 1) * TILE, TILE), TILE)
                 tile = tiles[slot].T
                 dense_ref[rows, columns] += jnp.where(slot < count, tile, jnp.zeros_like(tile))
 
@@ -123,7 +132,6 @@
     c = lax.axis_index("col")
     x, z_lo, y = r // 8, (r // 4) % 2, r % 4
     z_hi, core = c // 2, c % 2
-    my_place = place_of(x, z_lo, y)
 
     barrier = pltpu.get_barrier_semaphore()
 
@@ -141,13 +149,13 @@
             barrier, inc=1, device_id={"row": row_of(x, 1 - z_lo, y), "col": to}, device_id_type=MESH
         )
 
-    def product(buffer, chunks, side):
+    def product(tiles, chunks, side):
         columns = slice(side * SIDE, (side + 1) * SIDE)
         total = None
-        for at_x, at_y in chunks:
-            index = at_x * 4 + at_y
-            rows = pl.ds(pl.multiple_of(index * 2 * TILE, 2 * TILE), 2 * TILE)
-            source = jnp.concatenate([panel[buffer, index * 2], panel[buffer, index * 2 + 1]], axis=1)
+        for step_x, step_y in chunks:
+            index = step_x * 4 + step_y
+            rows = slice(index * 2 * TILE, (index + 1) * 2 * TILE)
+            source = jnp.concatenate([tiles[index * 2], tiles[index * 2 + 1]], axis=1)
             term = jnp.dot(source, dense[rows, columns], preferred_element_type=jnp.float32)
             total = term if total is None else total + term
         return total
@@ -156,54 +164,47 @@
         start, size = PARTS[part]
         return panel.at[buffer, place, pl.ds(start, size)]
 
-    def tile_copy(buffer, place, part, to_x, to_z, to_y):
+    def tile_copy(buffer, part, tile, to):
+        there = place_of(*(i - j for i, j in zip(tile, to)))
         return pltpu.make_async_remote_copy(
-            src_ref=part_of(buffer, place, part),
-            dst_ref=part_of(buffer, place, part),
+            src_ref=part_of(buffer, place_of(*tile), part),
+            dst_ref=part_of(buffer, there, part),
             send_sem=tile_send,
-            recv_sem=tile_recv.at[buffer, part, place],
-            device_id={"row": row_of(to_x, to_z, to_y), "col": c},
+            recv_sem=tile_recv.at[buffer, part, there],
+            device_id={"row": row_of((x + to[0]) % 4, (z_lo + to[2]) % 2, (y + to[1]) % 4), "col": c},
             device_id_type=MESH,
         )
 
-    def wait_tile(buffer, place, part):
-        ref = part_of(buffer, place, part)
-        pltpu.make_async_copy(ref, ref, tile_recv.at[buffer, part, place]).wait()
+    def wait_tile(buffer, part, tile):
+        ref = part_of(buffer, place_of(*tile), part)
+        pltpu.make_async_copy(ref, ref, tile_recv.at[buffer, part, place_of(*tile)]).wait()
 
     def at(part, along, across, z):
-        ahead, side = ((x, y), (y, x))[part]
-        ahead, side = (ahead + along) % 4, (side + across) % 4
-        return (ahead, (z_lo + z) % 2, side) if part == 0 else (side, (z_lo + z) % 2, ahead)
-
-    def flat(step_x, step_y, z):
-        return (x + step_x) % 4, (z_lo + z) % 2, (y + step_y) % 4
-
-    def send_along(buffer, place, part):
+        return (along, across, z) if part == 0 else (across, along, z)
+
+    def send_along(buffer, part, tile):
         for along in (1, 3, 2):
-            tile_copy(buffer, place, part, *at(part, along, 0, 0)).start()
+            tile_copy(buffer, part, tile, at(part, along, 0, 0)).start()
 
     def start_routed(buffer, part):
         for across, z in PLANE:
-            tile_copy(buffer, my_place, part, *at(part, 0, across, z)).start()
-        send_along(buffer, my_place, part)
+            tile_copy(buffer, part, (0, 0, 0), at(part, 0, across, z)).start()
+        send_along(buffer, part, (0, 0, 0))
 
     def start_flat(buffer):
-        tile_copy(buffer, my_place, 2, *flat(0, 0, 1)).start()
-        for step_x, step_y in FLAT:
-            tile_copy(buffer, my_place, 2, *flat(step_x, step_y, 0)).start()
+        tile_copy(buffer, 2, (0, 0, 0), (0, 0, 1)).start()
+        for step in FLAT:
+            tile_copy(buffer, 2, (0, 0, 0), (*step, 0)).start()
 
     def gather(buffer, wait_sends):
         with jax.named_scope("routed"):
-            for across, z in PLANE:
-                for part in range(2):
-                    place = place_of(*at(part, 0, across, z))
-                    wait_tile(buffer, place, part)
-                    send_along(buffer, place, part)
+            for part, across, z in RELAYS:
+                wait_tile(buffer, part, at(part, 0, across, z))
+                send_along(buffer, part, at(part, 0, across, z))
         with jax.named_scope("flat"):
-            for step_x, step_y in FLAT:
-                place = place_of(*flat(step_x, step_y, 0))
-                wait_tile(buffer, place, 2)
-                tile_copy(buffer, place, 2, *flat(0, 0, 1)).start()
+            for step in FLAT:
+                wait_tile(buffer, 2, (*step, 0))
+                tile_copy(buffer, 2, (*step, 0), (0, 0, 1)).start()
         for number, group in enumerate(GROUPS):
             with jax.named_scope("wait_group_%d" % number):
                 wait_group(buffer, group)
@@ -211,32 +212,28 @@
                     wait_sends()
             if number < len(GROUPS) - 1:
                 with jax.named_scope("mm_group_%d" % number):
-                    chunks = [spot(*step) for step in group]
                     for side in range(2):
                         if number == 0:
-                            partial[side] = product(buffer, chunks, side)
+                            partial[side] = product(panel.at[buffer], group, side)
                         else:
-                            partial[side] += product(buffer, chunks, side)
-        return [spot(*step) for step in GROUPS[-1]]
-
-    def spot(step_x, step_y):
-        return (x + step_x) % 4, (y + step_y) % 4
+                            partial[side] += product(panel.at[buffer], group, side)
 
     def wait_group(buffer, steps):
-        for step_x, step_y in steps:
+        for step in steps:
             for z in range(2):
-                if step_x:
-                    wait_tile(buffer, place_of(*at(0, step_x, step_y, z)), 0)
-                if step_y:
-                    wait_tile(buffer, place_of(*at(1, step_y, step_x, z)), 1)
-            wait_tile(buffer, place_of(*flat(step_x, step_y, 1)), 2)
-
-    def core_copy(buffer, half):
+                if step[0]:
+                    wait_tile(buffer, 0, (*step, z))
+                if step[1]:
+                    wait_tile(buffer, 1, (*step, z))
+            wait_tile(buffer, 2, (*step, 1))
+
+    def core_copy(buffer, half, part):
+        columns = pl.ds(pl.multiple_of(part * TILE, TILE), TILE)
         return pltpu.make_async_remote_copy(
-            src_ref=partial.at[OTHER, pl.ds(half * HALF, HALF)],
-            dst_ref=from_core.at[buffer, half],
-            send_sem=core_send.at[half],
-            recv_sem=core_recv.at[buffer, half],
+            src_ref=partial.at[OTHER, pl.ds(half * HALF, HALF), columns],
+            dst_ref=from_core.at[buffer, half, part],
+            send_sem=core_send.at[half, part],
+            recv_sem=core_recv.at[buffer, half, part],
             device_id={"row": r, "col": z_hi * 2 + 1 - core},
             device_id_type=MESH,
         )
@@ -258,11 +255,11 @@
         return steps, middle
 
     def both_cores(buffer, half, part):
+        core_copy(buffer, half, part).wait_recv()
         columns = pl.ds(pl.multiple_of(part * TILE, TILE), TILE)
-        return partial[OWN, half * HALF : (half + 1) * HALF, columns] + from_core[buffer, half, :, columns]
+        return partial[OWN, half * HALF : (half + 1) * HALF, columns] + from_core[buffer, half, part]
 
     def combine(level, buffer, half):
-        core_copy(buffer, half).wait_recv()
         steps, middle = code_scale(level)
         for step in (2, 1, 3):
             value = both_cores(buffer, half, (z_hi + step) % 4)
@@ -285,7 +282,8 @@
 
     def wait_sends():
         for half in range(2):
-            core_copy(0, half).wait_send()
+            for part in range(4):
+                core_copy(0, half, part).wait_send()
             for step in (1, 2, 3):
                 z_copy(0, half, step).wait_send()
 
@@ -293,21 +291,42 @@
         sent = panel.at[buffer, pl.ds(0, SRCS - 1)]
         pltpu.make_async_copy(sent, sent, tile_send).wait()
 
-    def reduce_level(level, buffer, out, side_product, drain, keep):
-        with jax.named_scope("mm_last"):
+    def reduce_level(level, buffer, out, side_product, drain, keep, early_core):
+        def other_side():
             partial[OTHER] = side_product(OTHER)
             for half in range(2):
-                core_copy(buffer, half).start()
+                for step in (2, 1, 3, 0):
+                    core_copy(buffer, half, (z_hi + step) % 4).start()
+
+        def own_side():
             partial[OWN] = side_product(OWN)
-        with jax.named_scope("combine"):
+
+        def combine_both():
             for half in range(2):
                 combine(level, buffer, half)
+
+        def own_first():
+            own_side()
+            combine_both()
+            other_side()
+
+        def other_first():
+            other_side()
+            own_side()
+            combine_both()
+
+        with jax.named_scope("mm_last"):
+            if early_core is None:
+                other_first()
+            else:
+                pl.when(core == early_core)(other_first)
+                pl.when(core != early_core)(own_first)
             drain()
         for half in range(2):
             with jax.named_scope("finish_%d" % half):
                 raw = finish(level, buffer, half)
                 if out is not None:
-                    panel[out, my_place, half * HALF : (half + 1) * HALF] = (raw * SHRINK).astype(jnp.bfloat16)
+                    panel[out, 0, half * HALF : (half + 1) * HALF] = (raw * SHRINK).astype(jnp.bfloat16)
                     start_routed(out, half)
                     if half == 1:
                         start_flat(out)
@@ -355,21 +374,18 @@
         early[...] = jnp.zeros_like(early)
         depth[...] = jnp.broadcast_to(depth_ref[...], (TILE, PANEL)).astype(jnp.float32).T.astype(jnp.int32)
         ids = jnp.broadcast_to(ids_ref[...], (TILE, PANEL)).astype(jnp.float32).T.astype(jnp.int32)
-
-        @pl.loop(0, SRCS)
-        def _(row):
-            place = place_of(row // 8, (row // 4) % 2, row % 4)
-            vertex = (row * N_COL + c) * TILE + lax.broadcasted_iota(jnp.int32, (PANEL, TILE), 1)
-            panel[0, place] = (vertex == ids).astype(jnp.float32).astype(jnp.bfloat16)
+        offsets = ids - lax.broadcasted_iota(jnp.int32, (PANEL, TILE), 1)
+
+        @pl.loop(0, SRCS // 4)
+        def _(quad):
+            for inner in range(4):
+                step_x, step_y = quad // 2, quad % 2 * 2 + inner // 2
+                row = row_of((x + step_x) % 4, (z_lo + inner) % 2, (y + step_y) % 4)
+                hit = offsets == (row * N_COL + c) * TILE
+                panel[0, quad * 4 + inner] = hit.astype(jnp.float32).astype(jnp.bfloat16)
 
     def first_product(side):
-        partial[side] = product(0, [(0, j) for j in range(4)], side)
-
-        @pl.loop(1, 3)
-        def _(at_x):
-            partial[side] += product(0, [(at_x, j) for j in range(4)], side)
-
-        total = partial[side] + product(0, [(3, j) for j in range(4)], side)
+        total = product(panel.at[0], [(i, j) for i in range(4) for j in range(4)], side)
         if side == OTHER:
             with jax.named_scope("barrier"):
                 pl.semaphore_wait(barrier, N_ROW - 1 + 2 * (N_COL - 1))
@@ -381,19 +397,20 @@
 
         return keep
 
-    reduce_level(1, 1, 1, first_product, lambda: None, keep_early(1))
+    reduce_level(1, 1, 1, first_product, lambda: None, keep_early(1), None)
 
     @pl.loop(2, LEVELS)
     def _(level):
         buffer = (level + 1) % 2
-        chunks = gather(buffer, wait_sends)
+        gather(buffer, wait_sends)
         reduce_level(
             level,
             1 - buffer,
             1 - buffer,
-            lambda side: partial[side] + product(buffer, chunks, side),
+            lambda side: partial[side] + product(panel.at[buffer], GROUPS[-1], side),
             lambda: wait_tile_sends(buffer),
             keep_early(level),
+            1,
         )
 
     norm_start(0, early, early_z, z_peer, mine_z)
@@ -404,7 +421,7 @@
         early[...] = norm_wait(0, early_z, z_peer)
         norm_start(1, early, early_xy, xy_peer, mine_xy)
 
-    chunks = gather(buffer, middle_of_last)
+    gather(buffer, middle_of_last)
 
     def keep_last(squares):
         last[...] = squares
@@ -413,9 +430,10 @@
         LEVELS,
         1 - buffer,
         None,
-        lambda side: partial[side] + product(buffer, chunks, side),
+        lambda side: partial[side] + product(panel.at[buffer], GROUPS[-1], side),
         lambda: wait_tile_sends(buffer),
         keep_last,
+        1,
     )
 
     with jax.named_scope("norm_z"):
@@ -472,7 +490,7 @@
             pltpu.VMEM((2, SRCS, TILE, PANEL), jnp.bfloat16),
             pltpu.VMEM((PANEL, TILE), jnp.int32),
             pltpu.VMEM((2, PANEL, SIDE), jnp.float32),
-            pltpu.VMEM((2, 2, HALF, SIDE), jnp.float32),
+            pltpu.VMEM((2, 2, 4, HALF, TILE), jnp.float32),
             pltpu.VMEM((2, 3, HALF, PANEL), jnp.int16),
             pltpu.VMEM((2, 2, 3, HALF, PANEL), jnp.int16),
             pltpu.VMEM((LEVELS, TILE, PANEL), jnp.float32),
@@ -484,8 +502,8 @@
             pltpu.VMEM((16, 1, PANEL), jnp.float32),
             pltpu.SemaphoreType.DMA,
             pltpu.SemaphoreType.DMA((2, 3, SRCS)),
-            pltpu.SemaphoreType.DMA((2,)),
-            pltpu.SemaphoreType.DMA((2, 2)),
+            pltpu.SemaphoreType.DMA((2, 4)),
+            pltpu.SemaphoreType.DMA((2, 2, 4)),
             pltpu.SemaphoreType.DMA((2, 3)),
             pltpu.SemaphoreType.DMA((2, 2, 3)),
             pltpu.SemaphoreType.DMA((4,)),

time: 122 us -> 121 us (level)
  Pallas kernels: 120 us -> 118 us
    pallas_call x1, Pallas kernels: 4.49 us -> 2.25 us  [local(): pl.pallas_call(densify, out_shape=pltpu.VMEM((SRCS * TILE, DESTS * TILE),...]
where the time goes in v5:
time: 121 us
  Pallas kernels  118 us (98%)
  between operations  1.34 us (1%)
  local copies, waits for them, and re-layouts  1.23 us (1%)
    pallas_call x1, Pallas kernels, local(): pl.pallas_call(levels_kernel, out_shape=(jax.ShapeDtypeStruct((TILE, PANE...  116 us

profile of v5, /device:TPU:1, one launch (start us, length us, event | category | flops | bytes accessed | tf_op | source)
XLA Modules:
  0.0 120.7 jit_solution(12019649673721835909)
XLA Ops:
  0.6 0.0 copy-start.1
  0.6 0.0 copy-start
  1.3 2.2 %densify.1.dense = bf16[4096,1024]{1,0:T(8,128)(2,1)S(1)} custom-call(s32[1,1]{1,0:T(1,128)S(6)} %copy.10.count_hbm, s32[1,1,128]{2,1,0:T(1,128)} %rows_hbm.1, s32[1,1,128]{2,1,0:T(1,128)} %cols_hbm.1, bf16[1,1,128,128,128]{4,3,2,1,0:T(8,128)(2,1)} %tiles_hbm.1), custom_call_target="tpu_custom_call" | custom-call | tf_op jit(solution)/shard_map/densify/pallas_call | solution.py:465
  3.6 0.0 copy-done.1
  3.6 0.0 copy-done
  3.6 115.9 %levels.1 = (f32[128,128]{1,0:T(8,128)S(1)}, f32[6,128]{1,0:T(8,128)S(1)}) custom-call(bf16[4096,1024]{1,0:T(8,128)(2,1)S(1)} %densify.1.dense, s32[1,128]{1,0:T(1,128)S(1)} %copy-done, s32[1,128]{1,0:T(1,128)S(1)} %bitcast.1), custom_call_target="tpu_custom_call" | custom-call | tf_op jit(solution)/shard_map/levels/pallas_call | solution.py:481
  119.5 0.6 copy.11
  120.1 0.6 copy.12
Async XLA Ops:
  0.6 2.9 %copy-start.1 = (s32[128]{0:T(128)S(1)}, s32[128]{0:T(128)}, u32[]{:S(2)}) copy-start(s32[128]{0:T(128)} %param.11) | copy-start | bytes 1540
  0.6 2.9 %copy-start = (s32[1,128]{1,0:T(1,128)S(1)}, s32[1,128]{1,0:T(1,128)}, u32[]{:S(2)}) copy-start(s32[1,128]{1,0:T(1,128)} %depth_ref.1) | copy-start | bytes 1540

commit v6 on v5

--- a/solution.py
+++ b/solution.py
@@ -7,7 +7,8 @@
 
 MESH = pl.DeviceIdType.MESH
 TILE = 128
-HALF = 64
+PIECES = ((0, 48), (48, 80))
+LONGEST = 80
 PANEL = 128
 LEVELS = 6
 KMAX = 128
@@ -104,15 +105,14 @@
     dense,
     depth_ref,
     ids_ref,
-    sums_ref,
-    logs_ref,
+    paths,
+    totals_ref,
     panel,
     depth,
     partial,
     from_core,
     codes,
     from_z,
-    paths,
     early,
     early_z,
     early_xy,
@@ -230,8 +230,8 @@
     def core_copy(buffer, half, part):
         columns = pl.ds(pl.multiple_of(part * TILE, TILE), TILE)
         return pltpu.make_async_remote_copy(
-            src_ref=partial.at[OTHER, pl.ds(half * HALF, HALF), columns],
-            dst_ref=from_core.at[buffer, half, part],
+            src_ref=partial.at[OTHER, pl.ds(*PIECES[half]), columns],
+            dst_ref=from_core.at[buffer, half, part, pl.ds(0, PIECES[half][1])],
             send_sem=core_send.at[half, part],
             recv_sem=core_recv.at[buffer, half, part],
             device_id={"row": r, "col": z_hi * 2 + 1 - core},
@@ -240,8 +240,8 @@
 
     def z_copy(buffer, half, step):
         return pltpu.make_async_remote_copy(
-            src_ref=codes.at[half, step - 1],
-            dst_ref=from_z.at[buffer, half, step - 1],
+            src_ref=codes.at[half, step - 1, pl.ds(0, PIECES[half][1])],
+            dst_ref=from_z.at[buffer, half, step - 1, pl.ds(0, PIECES[half][1])],
             send_sem=z_send.at[half, step - 1],
             recv_sem=z_recv.at[buffer, half, step - 1],
             device_id={"row": r, "col": ((z_hi + step) % 4) * 2 + core},
@@ -257,14 +257,14 @@
     def both_cores(buffer, half, part):
         core_copy(buffer, half, part).wait_recv()
         columns = pl.ds(pl.multiple_of(part * TILE, TILE), TILE)
-        return partial[OWN, half * HALF : (half + 1) * HALF, columns] + from_core[buffer, half, part]
+        return partial[OWN, pl.ds(*PIECES[half]), columns] + from_core[buffer, half, part, : PIECES[half][1]]
 
     def combine(level, buffer, half):
         steps, middle = code_scale(level)
         for step in (2, 1, 3):
             value = both_cores(buffer, half, (z_hi + step) % 4)
             code = jnp.round((jnp.log2(jnp.maximum(value, 2.0**-60)) - middle) * steps).astype(jnp.int32)
-            codes[half, step - 1] = jnp.where(value > 0.0, code, ZERO_CODE).astype(jnp.int16)
+            codes[half, step - 1, : PIECES[half][1]] = jnp.where(value > 0.0, code, ZERO_CODE).astype(jnp.int16)
             z_copy(buffer, half, step).start()
 
     def finish(level, buffer, half):
@@ -272,10 +272,10 @@
         mine = both_cores(buffer, half, z_hi)
         for step in (1, 3, 2):
             z_copy(buffer, half, step).wait_recv()
-            code = from_z[buffer, half, step - 1].astype(jnp.int32)
+            code = from_z[buffer, half, step - 1, : PIECES[half][1]].astype(jnp.int32)
             value = jnp.exp2(code.astype(jnp.float32) * (1.0 / steps) + middle)
             mine = mine + jnp.where(code == ZERO_CODE, 0.0, value)
-        rows = slice(half * HALF, (half + 1) * HALF)
+        rows = pl.ds(*PIECES[half])
         raw = jnp.where(depth[rows] >= level, mine, 0.0)
         paths[level - 1, rows] = raw
         return raw
@@ -326,7 +326,7 @@
             with jax.named_scope("finish_%d" % half):
                 raw = finish(level, buffer, half)
                 if out is not None:
-                    panel[out, 0, half * HALF : (half + 1) * HALF] = (raw * SHRINK).astype(jnp.bfloat16)
+                    panel[out, 0, pl.ds(*PIECES[half])] = (raw * SHRINK).astype(jnp.bfloat16)
                     start_routed(out, half)
                     if half == 1:
                         start_flat(out)
@@ -445,18 +445,22 @@
         norm_start(3, last, last_xy, xy_peer, mine_xy)
         last_total = norm_wait(3, last_xy, xy_peer)
 
-    with jax.named_scope("outputs"):
-        vertex = (r * N_COL + c) * TILE + lax.broadcasted_iota(jnp.int32, (TILE, PANEL), 0)
-        sums = (vertex == ids_ref[...]).astype(jnp.float32)
-        kappa = jnp.ones((1, PANEL), jnp.float32)
-        for level in range(LEVELS):
-            total = totals[level : level + 1] if level < LEVELS - 1 else last_total
-            mean_square = total / VERTICES / kappa / kappa + EPSILON
-            scale = kappa * jnp.sqrt(mean_square)
-            sums = sums + paths[level] * (1.0 / scale)
-            logs_ref[level : level + 1, :] = 0.5 * jnp.log(mean_square)
-            kappa = scale * SHRINK
-        sums_ref[...] = sums
+    totals_ref[0 : LEVELS - 1, :] = totals[0 : LEVELS - 1]
+    totals_ref[LEVELS - 1 : LEVELS, :] = last_total
+
+
+def outputs(ids_ref, paths, totals, sums_ref, logs_ref):
+    position = lax.axis_index("row") * N_COL + lax.axis_index("col")
+    vertex = position * TILE + lax.broadcasted_iota(jnp.int32, (TILE, PANEL), 0)
+    sums = (vertex == ids_ref[...]).astype(jnp.float32)
+    kappa = jnp.ones((1, PANEL), jnp.float32)
+    for level in range(LEVELS):
+        mean_square = totals[level : level + 1] / VERTICES / kappa / kappa + EPSILON
+        scale = kappa * jnp.sqrt(mean_square)
+        sums = sums + paths[level] * (1.0 / scale)
+        logs_ref[level : level + 1, :] = 0.5 * jnp.log(mean_square)
+        kappa = scale * SHRINK
+    sums_ref[...] = sums
 
 
 def local(adj_tiles, tile_rows, tile_cols, tile_count, tile_depth, source_ids):
@@ -478,11 +482,12 @@
         compiler_params=pltpu.CompilerParams(vmem_limit_bytes=53 * 2**20),
         name="densify",
     )(tile_count, tile_rows, tile_cols, adj_tiles)
-    return pl.pallas_call(
+    ids = source_ids.reshape(1, PANEL)
+    paths, totals = pl.pallas_call(
         levels_kernel,
         out_shape=(
-            jax.ShapeDtypeStruct((TILE, PANEL), jnp.float32),
-            jax.ShapeDtypeStruct((LEVELS, PANEL), jnp.float32),
+            pltpu.VMEM((LEVELS, TILE, PANEL), jnp.float32),
+            pltpu.VMEM((LEVELS, PANEL), jnp.float32),
         ),
         in_specs=[vmem, vmem, vmem],
         out_specs=(vmem, vmem),
@@ -490,10 +495,9 @@
             pltpu.VMEM((2, SRCS, TILE, PANEL), jnp.bfloat16),
             pltpu.VMEM((PANEL, TILE), jnp.int32),
             pltpu.VMEM((2, PANEL, SIDE), jnp.float32),
-            pltpu.VMEM((2, 2, 4, HALF, TILE), jnp.float32),
-            pltpu.VMEM((2, 3, HALF, PANEL), jnp.int16),
-            pltpu.VMEM((2, 2, 3, HALF, PANEL), jnp.int16),
-            pltpu.VMEM((LEVELS, TILE, PANEL), jnp.float32),
+            pltpu.VMEM((2, 2, 4, LONGEST, TILE), jnp.float32),
+            pltpu.VMEM((2, 3, LONGEST, PANEL), jnp.int16),
+            pltpu.VMEM((2, 2, 3, LONGEST, PANEL), jnp.int16),
             pltpu.VMEM((8, PANEL), jnp.float32),
             pltpu.VMEM((16, 8, PANEL), jnp.float32),
             pltpu.VMEM((16, 8, PANEL), jnp.float32),
@@ -513,7 +517,18 @@
             collective_id=0, has_side_effects=True, vmem_limit_bytes=32 * 2**20
         ),
         name="levels",
-    )(dense, tile_depth, source_ids.reshape(1, PANEL))
+    )(dense, tile_depth, ids)
+    return pl.pallas_call(
+        outputs,
+        out_shape=(
+            pltpu.HBM((TILE, PANEL), jnp.float32),
+            pltpu.HBM((LEVELS, PANEL), jnp.float32),
+        ),
+        in_specs=[vmem, vmem, vmem],
+        out_specs=(vmem, vmem),
+        compiler_params=pltpu.CompilerParams(vmem_limit_bytes=32 * 2**20),
+        name="outputs",
+    )(ids, paths, totals)
 
 
 def solution(mesh):

time: 121 us -> 120 us (level)
  local copies, waits for them, and re-layouts: 1.23 us -> 0.01 us
    unnamed x6 -> x4, local copies, waits for them, and re-layouts: 1.23 us -> 0.01 us
    pallas_call x1 -> x2, Pallas kernels: 116 us -> 116 us  [the longest x1 115 us: local(): pl.pallas_call(levels_kernel, out_shape=(pltpu.VMEM((LEVELS, TILE, PANEL)...]
where the time goes in v6:
time: 120 us; the launch traced here: 119 us
  Pallas kernels  118 us (98%)
  between operations  1.34 us (1%)
    pallas_call x1, Pallas kernels, local(): pl.pallas_call(levels_kernel, out_shape=(pltpu.VMEM((LEVELS, TILE, PANEL)...  115 us

profile of v6, /device:TPU:1, one launch (start us, length us, event | category | flops | bytes accessed | tf_op | source)
XLA Modules:
  0.0 119.3 jit_solution(7521899364231036450)
XLA Ops:
  0.6 0.0 copy-start
  0.6 0.0 copy-start.1
  1.3 2.3 %densify.1.dense = bf16[4096,1024]{1,0:T(8,128)(2,1)S(1)} custom-call(s32[1,1]{1,0:T(1,128)S(6)} %copy.8.count_hbm, s32[1,1,128]{2,1,0:T(1,128)} %rows_hbm.1, s32[1,1,128]{2,1,0:T(1,128)} %cols_hbm.1, bf16[1,1,128,128,128]{4,3,2,1,0:T(8,128)(2,1)} %tiles_hbm.1), custom_call_target="tpu_custom_call" | custom-call | tf_op jit(solution)/shard_map/densify/pallas_call | solution.py:469
  3.6 0.0 copy-done
  3.6 0.0 copy-done.1
  3.6 115.0 %levels.1 = (f32[6,128,128]{2,1,0:T(8,128)S(1)}, f32[6,128]{1,0:T(8,128)S(1)}) custom-call(bf16[4096,1024]{1,0:T(8,128)(2,1)S(1)} %densify.1.dense, s32[1,128]{1,0:T(1,128)S(1)} %copy-done.1, s32[1,128]{1,0:T(1,128)S(1)} %bitcast.1), custom_call_target="tpu_custom_call" | custom-call | tf_op jit(solution)/shard_map/levels/pallas_call | solution.py:486
  118.6 0.8 outputs.1
Async XLA Ops:
  0.6 3.0 %copy-start = (s32[128]{0:T(128)S(1)}, s32[128]{0:T(128)}, u32[]{:S(2)}) copy-start(s32[128]{0:T(128)} %param.11) | copy-start | bytes 1540
  0.6 3.0 %copy-start.1 = (s32[1,128]{1,0:T(1,128)S(1)}, s32[1,128]{1,0:T(1,128)}, u32[]{:S(2)}) copy-start(s32[1,128]{1,0:T(1,128)} %depth_ref.1) | copy-start | bytes 1540

commit v7 on v6

--- a/solution.py
+++ b/solution.py
@@ -135,19 +135,15 @@
 
     barrier = pltpu.get_barrier_semaphore()
 
-    @pl.loop(1, N_ROW)
-    def _(step):
-        pl.semaphore_signal(
-            barrier, inc=1, device_id={"row": (r + step) % N_ROW, "col": c}, device_id_type=MESH
-        )
-
-    @pl.loop(1, N_COL)
-    def _(step):
-        to = (c + step) % N_COL
-        pl.semaphore_signal(barrier, inc=1, device_id={"row": r, "col": to}, device_id_type=MESH)
-        pl.semaphore_signal(
-            barrier, inc=1, device_id={"row": row_of(x, 1 - z_lo, y), "col": to}, device_id_type=MESH
-        )
+    greeted = [(i, j, k, 0) for i in range(4) for j in range(4) for k in range(2) if i or j or k]
+    greeted += [(0, 0, k, m) for k in range(2) for m in range(1, N_COL)]
+
+    def hops(steps):
+        return sum(min(i, 4 - i) for i in steps[:2]) + steps[2] + 2 * min(steps[3] // 2, 4 - steps[3] // 2)
+
+    for i, j, k, m in sorted(greeted, key=hops, reverse=True):
+        to = {"row": row_of((x + i) % 4, (z_lo + k) % 2, (y + j) % 4), "col": (c + m) % N_COL}
+        pl.semaphore_signal(barrier, inc=1, device_id=to, device_id_type=MESH)
 
     def product(tiles, chunks, side):
         columns = slice(side * SIDE, (side + 1) * SIDE)

time: 120 us -> 119 us (level)
  no operation moved by 1% of the time
where the time goes in v7:
time: 119 us
  Pallas kernels  118 us (99%)
  between operations  1.34 us (1%)
    pallas_call x1, Pallas kernels, local(): pl.pallas_call(levels_kernel, out_shape=(pltpu.VMEM((LEVELS, TILE, PANEL)...  115 us

profile of v7, /device:TPU:1, one launch (start us, length us, event | category | flops | bytes accessed | tf_op | source)
XLA Modules:
  0.0 119.3 jit_solution(18148439905903322871)
XLA Ops:
  0.6 0.0 copy-start
  0.6 0.0 copy-start.1
  1.3 2.2 %densify.1.dense = bf16[4096,1024]{1,0:T(8,128)(2,1)S(1)} custom-call(s32[1,1]{1,0:T(1,128)S(6)} %copy.8.count_hbm, s32[1,1,128]{2,1,0:T(1,128)} %rows_hbm.1, s32[1,1,128]{2,1,0:T(1,128)} %cols_hbm.1, bf16[1,1,128,128,128]{4,3,2,1,0:T(8,128)(2,1)} %tiles_hbm.1), custom_call_target="tpu_custom_call" | custom-call | tf_op jit(solution)/shard_map/densify/pallas_call | solution.py:465
  3.6 0.0 copy-done
  3.6 0.0 copy-done.1
  3.6 114.9 %levels.1 = (f32[6,128,128]{2,1,0:T(8,128)S(1)}, f32[6,128]{1,0:T(8,128)S(1)}) custom-call(bf16[4096,1024]{1,0:T(8,128)(2,1)S(1)} %densify.1.dense, s32[1,128]{1,0:T(1,128)S(1)} %copy-done.1, s32[1,128]{1,0:T(1,128)S(1)} %bitcast.1), custom_call_target="tpu_custom_call" | custom-call | tf_op jit(solution)/shard_map/levels/pallas_call | solution.py:482
  118.5 0.8 outputs.1
Async XLA Ops:
  0.6 2.9 %copy-start = (s32[128]{0:T(128)S(1)}, s32[128]{0:T(128)}, u32[]{:S(2)}) copy-start(s32[128]{0:T(128)} %param.11) | copy-start | bytes 1540
  0.6 2.9 %copy-start.1 = (s32[1,128]{1,0:T(1,128)S(1)}, s32[1,128]{1,0:T(1,128)}, u32[]{:S(2)}) copy-start(s32[1,128]{1,0:T(1,128)} %depth_ref.1) | copy-start | bytes 1540
